TPU v7x, 32 devices: a whole 2x2x4 slice. The times are simulated.
32 devices in a mesh: dom: 8 (over y, x, core), rep: 4 (over z).
Axes of the slice: x: 2, y: 2, z: 4, core: 2. Of those that a mesh axis runs over, the one named last changes fastest.
Arguments:
- hop_feats: bfloat16 [3, 65536, 128], P(None, ('dom', 'rep')), may hold values from -6 to 6
- adj_local: bfloat16 [512, 12, 128, 128], P(('dom', 'rep')), may hold values from -0.125 to 0.125
- local_cols: int32 [512, 12], P(('dom', 'rep')), may hold values from 0 to 15
- adj_halo: bfloat16 [512, 4, 128, 128], P(('dom', 'rep')), may hold values from -0.125 to 0.125
- halo_cols: int32 [512, 4], P(('dom', 'rep')), may hold values from 0 to 3
- boundary_rows: int32 [32, 512], P(('dom', 'rep')), may hold values from 0 to 2047
- train_ids: int32 [32, 2048], P(('dom', 'rep')), may hold values from 0 to 2047, as said below
- shuffle: int32 [32, 2048], P(('dom', 'rep')), may hold values from 0 to 2047, as said below
- labels: int32 [65536], P(('dom', 'rep')), may hold values from 0 to 171
- labelled: int32 [65536], P(('dom', 'rep')), may hold values from 0 to 1
- w_first: bfloat16 [512, 1024], P(None, 'rep'), may hold values from -1 to 1
- w_second: bfloat16 [1024, 172], P('rep'), may hold values from -2 to 2
Outputs:
- next_hop: bfloat16 [65536, 128], P(('dom', 'rep'))
- batch_loss: float32 [32, 32], P(('dom', 'rep'))
- grad_first: float32 [512, 1024], P('dom', 'rep')
- grad_second: float32 [1024, 172], P('rep')
Inputs may be any that keep to these rules, and one draw needn't show every extreme that they name: `local_cols`: local tile indices of the partition's own row tiles. `halo_cols`: indices of received boundary tiles. `boundary_rows`: rows of the sending partition itself. `train_ids`: rows of the partition itself. `shuffle`: each row is a permutation of 0 .. 2047.
All inputs are finite; a program needn't handle non-finite values.
Results may differ from a plain program's by a relative error of at most 0.005.
The roundings to bfloat16 on the way count: a program that leaves them out, or rounds other values in their place, can miss the bound.
Values may be sent and summed in bfloat16 or wider, within the bound.
A program may use at most 128 MiB of HBM per device.

v0:
```python
import functools

import jax
import jax.numpy as jnp
from jax import lax
from jax.experimental import pallas as pl
from jax.experimental.pallas import tpu as pltpu
from jax.sharding import PartitionSpec as P

F32 = jnp.float32
BF16 = jnp.bfloat16
BIG = 60 * 1024 * 1024


def where_am_i(ndom, nrep):
    return lax.axis_index("dom") * nrep + lax.axis_index("rep")


def enter(me, n, nrep):
    barrier = pltpu.get_barrier_semaphore()

    def greet(o, carry):
        peer = lax.rem(me + o, n)
        pl.semaphore_signal(barrier, inc=1, device_id=(peer // nrep, lax.rem(peer, nrep)),
                            device_id_type=pl.DeviceIdType.MESH)
        return carry

    lax.fori_loop(1, n, greet, 0)
    pl.semaphore_wait(barrier, n - 1)


def spread(me, n, nrep, src_at, dst, send_sem, recv_sem):
    def copy(o):
        peer = lax.rem(me + o, n)
        return pltpu.make_async_remote_copy(
            src_ref=src_at(peer), dst_ref=dst.at[me],
            send_sem=send_sem.at[o], recv_sem=recv_sem.at[o],
            device_id=(peer // nrep, lax.rem(peer, nrep)),
            device_id_type=pl.DeviceIdType.MESH)

    def start(o, carry):
        copy(o).start()
        return carry

    def finish(o, carry):
        copy(o).wait()
        return carry

    return (lambda: lax.fori_loop(1, n, start, 0)), (lambda: lax.fori_loop(1, n, finish, 0))


def comm_call(kernel, outs, scratch, name, cid, *args):
    return pl.pallas_call(
        kernel,
        out_shape=outs,
        in_specs=[pl.BlockSpec(memory_space=pltpu.VMEM)] * len(args),
        out_specs=jax.tree.map(lambda _: pl.BlockSpec(memory_space=pltpu.VMEM), outs),
        scratch_shapes=scratch,
        compiler_params=pltpu.CompilerParams(collective_id=cid, has_side_effects=True),
        name=name,
    )(*args)


def dma_sems(n, count):
    return [pltpu.SemaphoreType.DMA((n,))] * count


def halo_kernel(ndom, nrep, src, cnt, out, tot, buf, crow, cbuf, ssem, rsem, s2, r2):
    n = ndom * nrep
    me = where_am_i(ndom, nrep)
    crow[0] = cnt[...]
    enter(me, n, nrep)
    start, finish = spread(me, n, nrep, lambda p: src.at[p], buf, ssem, rsem)
    cstart, cfinish = spread(me, n, nrep, lambda p: crow.at[0], cbuf, s2, r2)
    start()
    cstart()
    buf[me] = src[me]
    cbuf[me] = cnt[...]
    finish()
    cfinish()
    out[...] = buf[...]
    tot[...] = jnp.maximum(jnp.sum(cbuf[...], axis=0), 1.0)


def stats_kernel(ndom, nrep, forward, chunk, src, row, out, turned, recv, gath, lrow, lbuf,
                 s1, r1, s2, r2, s3, r3):
    n = ndom * nrep
    me = where_am_i(ndom, nrep)
    if not forward:
        lrow[0] = row[...]
    enter(me, n, nrep)
    start, finish = spread(me, n, nrep, lambda p: src.at[p], recv, s1, r1)
    start()
    lstart, lfinish = spread(me, n, nrep, lambda p: lrow.at[0], lbuf, s3, r3)
    if not forward:
        lstart()
        lbuf[me] = row[...]
    recv[me] = src[me]
    finish()
    half = src.shape[1] // 2
    got = recv[...]
    first = jnp.sum(got[:, :half], axis=0)
    second = jnp.sum(got[:, half:], axis=0)
    scale = 1.0 / (n * chunk)
    if forward:
        mu = first * (1.0 / n)
        off = got[:, :half] - mu[None]
        m2 = second + chunk * jnp.sum(off * off, axis=0)
        result = jnp.concatenate([mu, lax.rsqrt(m2 * scale + 1e-05)], axis=0)
    else:
        result = jnp.concatenate([first * scale, second * scale], axis=0)
    gath[me] = result
    start, finish = spread(me, n, nrep, lambda p: gath.at[me], gath, s2, r2)
    start()
    if forward:
        turned[...] = jnp.zeros_like(turned)
    else:
        lfinish()
        losses = lbuf[...]
        source = lax.broadcasted_iota(jnp.int32, losses.shape, 0)
        lane = lax.broadcasted_iota(jnp.int32, losses.shape, 2)
        mine = jnp.sum(jnp.where(lane == me, losses, 0.0), axis=2, keepdims=True)
        turned[...] = jnp.sum(jnp.where(lane == source, mine, 0.0), axis=0)
    finish()
    out[...] = gath[...]


def grads_kernel(ndom, nrep, cores, split, src, out1, out2, recv0, sum0, recv1, sum1, kept, recv2, gath,
                 s0, r0, s1, r1, s2, r2, s3, r3):
    dom, rep = lax.axis_index("dom"), lax.axis_index("rep")
    me = dom * nrep + rep
    chips = ndom // cores
    chip, core = dom // cores, lax.rem(dom, cores)
    enter(me, ndom * nrep, nrep)

    def to(src_ref, dst_ref, ssem, rsem, peer_dom, peer_rep):
        return pltpu.make_async_remote_copy(
            src_ref=src_ref, dst_ref=dst_ref, send_sem=ssem, recv_sem=rsem,
            device_id=(peer_dom, peer_rep), device_id_type=pl.DeviceIdType.MESH)

    def run(copies):
        for copy in copies:
            copy.start()
        for copy in copies:
            copy.wait()

    other = cores - 1 - core
    run([to(src.at[other, a], recv0.at[a], s0.at[a], r0.at[a], chip * cores + other, rep)
         for a in range(chips)])
    sum0[...] = (src[core].astype(F32) + recv0[...].astype(F32)).astype(BF16)

    def near(o):
        peer = lax.rem(chip + o, chips)
        return to(sum0.at[peer], recv1.at[o - 1], s1.at[o], r1.at[o], peer * cores + core, rep)

    run([near(o) for o in range(1, chips)])
    total = src[core, chip].astype(F32) + recv0[chip].astype(F32)
    for o in range(1, chips):
        total = total + recv1[o - 1].astype(F32)
    sum1[...] = total.astype(BF16)
    kept[...] = total

    def along(o):
        peer = lax.rem(rep + o, nrep)
        return to(sum1.at[peer], recv2.at[o - 1], s2.at[o], r2.at[o], dom, peer)

    run([along(o) for o in range(1, nrep)])
    total = kept[rep]
    for o in range(1, nrep):
        total = total + recv2[o - 1].astype(F32)
    out1[...] = total[:split]
    gath[dom] = total[split:]
    run([to(gath.at[dom], gath.at[dom], s3.at[o], r3.at[o], lax.rem(dom + o, ndom), rep)
         for o in range(1, ndom)])
    out2[...] = gath[...]


def hop_kernel(kl, kh, lcols, hcols, adj_l, adj_h, own, halo, out):
    i = pl.program_id(0)
    left = jnp.concatenate([adj_l[0, k] for k in range(kl)] + [adj_h[0, k] for k in range(kh)], axis=1)
    right = jnp.concatenate(
        [own[0, lcols[i, k]] for k in range(kl)] + [halo[hcols[i, k]] for k in range(kh)], axis=0)
    out[0] = jnp.dot(left, right, preferred_element_type=F32).astype(BF16)


def batch_lanes(rows, wide, chunk):
    at = pl.program_id(0) * rows + lax.broadcasted_iota(jnp.int32, (rows, wide), 0)
    return at // chunk == lax.broadcasted_iota(jnp.int32, (rows, wide), 1)


def one_hot(column, count):
    lanes = lax.broadcasted_iota(jnp.int32, (column.shape[0], count), 1)
    return (lanes == column).astype(F32).astype(BF16)


def by_lanes(left, right):
    return lax.dot_general(left, right, (((1,), (1,)), ((), ())), preferred_element_type=F32)


def pick_kernel(chunk, shuf, bound, ids, labels, labelled, feats, x_out, tag_out, sent_out, cnt_out):
    rows = shuf.shape[0]
    nodes = feats.shape[1]
    sent_out[...] = jnp.dot(one_hot(bound[...], nodes), feats[2], preferred_element_type=F32).astype(BF16)
    numbers = ids[...]
    blank = jnp.zeros((6, nodes), F32)
    table = jnp.concatenate(
        [(numbers // 256).astype(F32), (numbers % 256).astype(F32), jnp.zeros((6, ids.shape[1]), F32)], axis=0)
    two = by_lanes(one_hot(shuf[...], ids.shape[1]), table.astype(BF16))
    order = two[:, 0:1] * 256.0 + two[:, 1:2]
    pick = one_hot(order.astype(jnp.int32), nodes)
    whole = jnp.concatenate([feats[0], feats[1], feats[2]], axis=1)
    x_out[...] = jnp.dot(pick, whole, preferred_element_type=F32).astype(BF16)
    marks = jnp.concatenate([labels[...].astype(F32), labelled[...].astype(F32), blank], axis=0)
    tags = by_lanes(pick, marks.astype(BF16))
    tag_out[:, 0:8] = tags
    tag_out[:, 8:9] = order

    @pl.when(pl.program_id(0) == 0)
    def _():
        cnt_out[...] = jnp.zeros_like(cnt_out)

    here = batch_lanes(rows, cnt_out.shape[1], chunk)
    cnt_out[...] += jnp.sum(jnp.where(here, tags[:, 1:2], 0.0), axis=0, keepdims=True)


def store_lines(out, at, value):
    for j in range(value.shape[2] // 128):
        out[:, at + j:at + j + 1] = value[:, :, j * 128:(j + 1) * 128]


def load_lines(ref, at, lines):
    return jnp.concatenate([ref[:, at + j:at + j + 1] for j in range(lines)], axis=2)


def pre_kernel(chunk, x3, tag, hop, w1, x_out, z_out, st_out):
    rows = x3.shape[0]
    order = tag[:, 8:9].astype(jnp.int32)
    got = jnp.dot(one_hot(order, hop.shape[0]), hop[...], preferred_element_type=F32)
    x = jnp.concatenate([x3[...], got.astype(BF16)], axis=1)
    x_out[...] = x
    z = jnp.concatenate(
        [jnp.dot(x, w1[r], preferred_element_type=F32) for r in range(w1.shape[0])], axis=1)
    z_out[...] = z
    z3 = z.reshape(rows // chunk, chunk, z.shape[1])
    mean = jnp.sum(z3, axis=1, keepdims=True) * (1.0 / chunk)
    off = z3 - mean
    store_lines(st_out, 0, mean)
    store_lines(st_out, st_out.shape[1] // 2, jnp.sum(off * off, axis=1, keepdims=True))


def head_kernel(chunk, z_ref, tag, st, counts, own_counts, w2, dl_out, g2_out, gs_out, loss_out):
    rows, hidden_units = z_ref.shape
    groups = rows // chunk
    half = st.shape[1] // 2
    z3 = z_ref[...].reshape(groups, chunk, hidden_units)
    normed = ((z3 - load_lines(st, 0, half)) * load_lines(st, half, half)).reshape(rows, hidden_units)
    hidden = jnp.maximum(normed, 0.0).astype(BF16)
    second = w2[...]
    logits = jnp.dot(hidden, second, preferred_element_type=F32)
    row_max = jnp.max(logits, axis=1, keepdims=True)
    expos = jnp.exp(logits - row_max)
    totals = jnp.sum(expos, axis=1, keepdims=True)
    target = tag[:, 0:1].astype(jnp.int32)
    mark = tag[:, 1:2]
    onehot = (lax.broadcasted_iota(jnp.int32, logits.shape, 1) == target).astype(F32)
    cross = jnp.log(totals) + row_max - jnp.sum(onehot * logits, axis=1, keepdims=True)
    here = batch_lanes(rows, counts.shape[1], chunk)
    count = jnp.sum(jnp.where(here, counts[...], 0.0), axis=1, keepdims=True)
    dlogits = ((expos / totals - onehot) * (mark / count)).astype(BF16)
    dl_out[...] = dlogits

    @pl.when(pl.program_id(0) == 0)
    def _():
        g2_out[...] = jnp.zeros_like(g2_out)
        loss_out[...] = jnp.zeros_like(loss_out)

    loss_out[...] += jnp.sum(jnp.where(here, mark * cross, 0.0), axis=0, keepdims=True)

    @pl.when(pl.program_id(0) == pl.num_programs(0) - 1)
    def _():
        loss_out[...] = loss_out[...] / jnp.maximum(own_counts[...], 1.0)

    g2_out[...] += lax.dot_general(hidden, dlogits, (((0,), (0,)), ((), ())), preferred_element_type=F32)
    masked = jnp.where(normed > 0, by_lanes(dlogits, second), 0.0)
    store_lines(gs_out, 0, jnp.sum(masked.reshape(groups, chunk, hidden_units), axis=1, keepdims=True))
    store_lines(gs_out, half, jnp.sum(
        (masked * normed).reshape(groups, chunk, hidden_units), axis=1, keepdims=True))


def tail_kernel(chunk, ndom, nrep, cores, z_ref, x_ref, st, gm, w2, dl, g2, out, acc):
    rows, hidden_units = z_ref.shape
    groups = rows // chunk
    half = st.shape[1] // 2
    z3 = z_ref[...].reshape(groups, chunk, hidden_units)
    rstd = load_lines(st, half, half)
    normed = (z3 - load_lines(st, 0, half)) * rstd
    back = by_lanes(dl[...], w2[...])
    masked = jnp.where(normed > 0, back.reshape(groups, chunk, hidden_units), 0.0)
    dpre = (masked - load_lines(gm, 0, half) - normed * load_lines(gm, half, half)) * rstd
    dpre = dpre.reshape(rows, hidden_units).astype(BF16)

    @pl.when(pl.program_id(0) == 0)
    def _():
        acc[...] = jnp.zeros_like(acc)

    acc[...] += lax.dot_general(x_ref[...], dpre, (((0,), (0,)), ((), ())), preferred_element_type=F32)

    @pl.when(pl.program_id(0) == pl.num_programs(0) - 1)
    def _():
        high, wide = acc.shape[0] // ndom, acc.shape[1] // nrep
        part, classes = g2.shape[0] // (ndom * nrep), g2.shape[1]
        for d in range(ndom):
            for r in range(nrep):
                first = acc[d * high:(d + 1) * high, r * wide:(r + 1) * wide]
                at = (r * ndom + d) * part
                second = jnp.concatenate(
                    [g2[at:at + part, :], jnp.zeros((part, wide - classes), F32)], axis=1)
                out[d % cores, d // cores, r] = jnp.concatenate([first, second], axis=0).astype(BF16)


def whole_spec(shape):
    return pl.BlockSpec(tuple(shape), lambda i: (0,) * len(shape))


def lead_spec(shape):
    return pl.BlockSpec(tuple(shape), lambda i: (i,) + (0,) * (len(shape) - 1))


def send_rep(half, nrep):
    return [lax.ppermute(half, "rep", [(s, (s + o) % nrep) for s in range(nrep)]) for o in range(1, nrep)]


def gather_rep(half, arrived, ndom, nrep, cores):
    dom, rep = lax.axis_index("dom"), lax.axis_index("rep")
    core = lax.rem(dom, cores)
    slots = jnp.zeros((nrep,) + half.shape, half.dtype)
    slots = lax.dynamic_update_slice(slots, half[None], (rep, 0, 0))
    for o in range(1, nrep):
        slots = lax.dynamic_update_slice(slots, arrived[o - 1][None], (lax.rem(rep - o + nrep, nrep), 0, 0))
    theirs = lax.ppermute(slots, "dom", [(d, d + 1 - 2 * (d % 2)) for d in range(ndom)])
    both = jnp.zeros((cores,) + slots.shape, slots.dtype)
    both = lax.dynamic_update_slice(both, slots[None], (core, 0, 0, 0))
    return lax.dynamic_update_slice(both, theirs[None], (cores - 1 - core, 0, 0, 0))


def shards(hop_feats, adj_local, local_cols, adj_halo, halo_cols, boundary_rows, train_ids,
           shuffle, labels, labelled, w_first, w_second):
    ndom, nrep = lax.axis_size("dom"), lax.axis_size("rep")
    n = ndom * nrep
    cores = 2
    row_tiles, kl, tile, _ = adj_local.shape
    kh = adj_halo.shape[1]
    rows, width = hop_feats.shape[1:]
    slots = train_ids.shape[1]
    hidden_units, classes = w_second.shape[0] * nrep, w_second.shape[1]
    chunk = slots // n
    block = 256
    steps = slots // block
    groups = block // chunk
    wide = -(-n // 128) * 128
    big = pltpu.CompilerParams(vmem_limit_bytes=BIG)
    sds = jax.ShapeDtypeStruct

    core = lax.rem(lax.axis_index("dom"), cores)
    own_cols = hidden_units // nrep
    h1, h2 = w_first.shape[0] // cores, w_second.shape[0] // cores
    half = jnp.concatenate([
        lax.dynamic_slice(w_first, (core * h1, 0), (h1, own_cols)),
        jnp.pad(lax.dynamic_slice(w_second, (core * h2, 0), (h2, classes)),
                ((0, 0), (0, own_cols - classes)))], axis=0)
    arrived = send_rep(half, nrep)

    sent_block = boundary_rows.shape[1] // steps
    x3, tags, sent, own_counts = pl.pallas_call(
        functools.partial(pick_kernel, chunk),
        out_shape=(sds((slots, 3 * width), BF16), sds((slots, 128), F32),
                   sds((boundary_rows.shape[1], width), BF16), sds((1, wide), F32)),
        grid=(steps,),
        in_specs=[lead_spec((block, 1)), lead_spec((sent_block, 1)), whole_spec((1, slots)),
                  whole_spec((1, rows)), whole_spec((1, rows)), whole_spec(hop_feats.shape)],
        out_specs=(lead_spec((block, 3 * width)), lead_spec((block, 128)),
                   lead_spec((sent_block, width)), whole_spec((1, wide))),
        compiler_params=big, name="pick",
        cost_estimate=pl.CostEstimate(flops=2 * slots * rows * 5 * width, bytes_accessed=4 << 20, transcendentals=0),
    )(shuffle[0][:, None], boundary_rows[0][:, None], train_ids, labels[None], labelled[None], hop_feats)

    arrived, own_counts = lax.optimization_barrier((arrived, own_counts))
    both = gather_rep(half, arrived, ndom, nrep, cores)
    sent = sent.reshape(n, -1, width)
    halo, counts = comm_call(
        functools.partial(halo_kernel, ndom, nrep), (sds(sent.shape, BF16), sds((1, wide), F32)),
        [pltpu.VMEM(sent.shape, BF16), pltpu.VMEM((1, 1, wide), F32), pltpu.VMEM((n, 1, wide), F32)]
        + dma_sems(n, 4), "halo", 1, sent, own_counts)
    halo = halo.reshape(-1, tile, width)

    next_hop = pl.pallas_call(
        functools.partial(hop_kernel, kl, kh),
        out_shape=sds((row_tiles, tile, width), BF16),
        grid=(row_tiles,),
        in_specs=[
            pl.BlockSpec(memory_space=pltpu.SMEM), pl.BlockSpec(memory_space=pltpu.SMEM),
            lead_spec((1, kl, tile, tile)), lead_spec((1, kh, tile, tile)),
            pl.BlockSpec((1, row_tiles, tile, width), lambda i: (2, 0, 0, 0)), whole_spec(halo.shape)],
        out_specs=lead_spec((1, tile, width)),
        compiler_params=big, name="hop",
        cost_estimate=pl.CostEstimate(flops=2 * rows * width * tile * (kl + kh), bytes_accessed=9 << 20, transcendentals=0),
    )(local_cols, halo_cols, adj_local, adj_halo, hop_feats.reshape(3, row_tiles, tile, width), halo)
    next_hop = next_hop.reshape(rows, width)

    w1 = both[:, :, :h1].transpose(1, 0, 2, 3).reshape(nrep, cores * h1, own_cols)
    w2 = both[:, :, h1:, :classes].transpose(1, 0, 2, 3).reshape(hidden_units, classes)

    lines = 2 * hidden_units // 128
    x, z, stats = pl.pallas_call(
        functools.partial(pre_kernel, chunk),
        out_shape=(sds((slots, 4 * width), BF16), sds((slots, hidden_units), F32),
                   sds((n, lines, 128), F32)),
        grid=(steps,),
        in_specs=[lead_spec((block, 3 * width)), lead_spec((block, 128)), whole_spec((rows, width)),
                  whole_spec(w1.shape)],
        out_specs=(lead_spec((block, 4 * width)), lead_spec((block, hidden_units)),
                   lead_spec((groups, lines, 128))),
        compiler_params=big, name="pre",
    )(x3, tags, next_hop, w1)

    def combine(values, row, forward, cid):
        return comm_call(
            functools.partial(stats_kernel, ndom, nrep, forward, chunk),
            (sds((n, lines, 128), F32), sds((1, wide), F32)),
            [pltpu.VMEM((n, lines, 128), F32)] * 2
            + [pltpu.VMEM((1, 1, wide), F32), pltpu.VMEM((n, 1, wide), F32)] + dma_sems(n, 6),
            "stats_f" if forward else "stats_b", cid, values, row)

    stats, _ = combine(stats, own_counts, True, 2)

    line_spec = lead_spec((groups, lines, 128))
    dlogits, grad_two, gsums, losses = pl.pallas_call(
        functools.partial(head_kernel, chunk),
        out_shape=(sds((slots, classes), BF16), sds((hidden_units, classes), F32),
                   sds((n, lines, 128), F32), sds((1, wide), F32)),
        grid=(steps,),
        in_specs=[lead_spec((block, hidden_units)), lead_spec((block, 128)), line_spec,
                  whole_spec((1, wide)), whole_spec((1, wide)), whole_spec((hidden_units, classes))],
        out_specs=(lead_spec((block, classes)), whole_spec((hidden_units, classes)), line_spec,
                   whole_spec((1, wide))),
        compiler_params=big, name="head",
    )(z, tags, stats, counts, own_counts, w2)

    gmeans, turned = combine(gsums, losses, False, 3)
    loss = turned[:, :n]

    own_rows, part = 4 * width // ndom, hidden_units // n
    size = (nrep, own_rows + part, own_cols)
    packed = pl.pallas_call(
        functools.partial(tail_kernel, chunk, ndom, nrep, cores),
        out_shape=sds((cores, ndom // cores) + size, BF16),
        grid=(steps,),
        in_specs=[lead_spec((block, hidden_units)), lead_spec((block, 4 * width)), line_spec, line_spec,
                  whole_spec((hidden_units, classes)), lead_spec((block, classes)),
                  whole_spec((hidden_units, classes))],
        out_specs=whole_spec((cores, ndom // cores) + size),
        scratch_shapes=[pltpu.VMEM((4 * width, hidden_units), F32)],
        compiler_params=big, name="tail",
    )(z, x, stats, gmeans, w2, dlogits, grad_two)

    chips = ndom // cores
    first, second = comm_call(
        functools.partial(grads_kernel, ndom, nrep, cores, own_rows),
        (sds((own_rows, own_cols), F32), sds((ndom, part, own_cols), F32)),
        [pltpu.VMEM((chips,) + size, BF16), pltpu.VMEM((chips,) + size, BF16),
         pltpu.VMEM((chips - 1,) + size, BF16), pltpu.VMEM(size, BF16), pltpu.VMEM(size, F32),
         pltpu.VMEM((nrep - 1,) + size[1:], BF16), pltpu.VMEM((ndom, part, own_cols), F32)]
        + dma_sems(chips, 4) + dma_sems(nrep, 2) + dma_sems(ndom, 2),
        "grads", 4, packed)
    second = second.reshape(ndom * part, own_cols)[:, :classes]
    return (next_hop, loss, first, second)


def solution(mesh):
    both = ("dom", "rep")
    placed = (
        P(None, both, None), P(both, None, None, None), P(both, None), P(both, None, None, None),
        P(both, None), P(both, None), P(both, None), P(both, None), P(both), P(both),
        P(None, "rep"), P("rep", None),
    )
    return jax.shard_map(
        shards, mesh=mesh, in_specs=placed,
        out_specs=(P(both, None), P(both, None), P("dom", "rep"), P("rep", None)),
        check_vma=False,
    )
```

profile of v0, /device:TPU:0, one launch (start us, length us, event | category | flops | bytes accessed | tf_op | source)
XLA Modules:
  0.0 170.5 jit_solution(17496240912202651530)
XLA Ops:
  0.7 0.8 constant_dynamic-slice_fusion
  1.5 0.1 copy.27
  1.7 5.1 %collective-permute-start.2 = (bf16[384,256]{1,0:T(8,128)(2,1)S(1)}, bf16[384,256]{1,0:T(8,128)(2,1)S(1)}, u32[]{:S(2)}, u32[]{:S(2)}) collective-permute-start(bf16[384,256]{1,0:T(8,128)(2,1)S(1)} %fusion.1), channel_id=1, source_target_pairs={{0,3},{1,0},{2,1},{3,2},{4,7},{5,4},{6,5},{7,6},{8,11},{9,8},{10,9... | collective-permute-start | bytes 589832 | tf_op jit(solution)/shard_map/ppermute | solution.py:330
  6.8 1.0 collective-permute-start
  7.8 1.5 copy.21.bound
  9.4 2.0 %copy.20.shuf = s32[2048,1]{1,0:T(8,128)} copy(s32[2048,1]{0,1:T(1,128)} %bitcast.40) | data formatting | bytes 16384 | tf_op jit(solution)/shard_map/broadcast_in_dim;squeeze | solution.py:385
  11.4 16.5 %pick.1 = (bf16[2048,384]{1,0:T(8,128)(2,1)}, f32[2048,128]{1,0:T(8,128)}, bf16[512,128]{1,0:T(8,128)(2,1)}, f32[1,128]{1,0:T(1,128)}) custom-call(s32[2048,1]{1,0:T(8,128)} %copy.20.shuf, s32[512,1]{1,0:T(8,128)} %copy.21.bound, s32[1,2048]{1,0:T(1,128)} %ids.1, s32[1,2048]{1,0:T(1,128)} %bitcast.42, s32[1,2048]{1,0:T(1,128)} %bitcast.43, ...), custom_call_target="tpu_custom_call" | custom-call | flops 5368709120 | bytes 4194304 | tf_op jit(solution)/shard_map/pick/pallas_call | solution.py:374
  28.1 0.1 collective-permute-start.3
  28.2 0.4 copy-done.1
  28.6 0.7 copy.23.hcols
  29.3 13.1 %halo.1 = (bf16[32,16,128]{2,1,0:T(8,128)(2,1)}, f32[1,128]{1,0:T(1,128)}) custom-call(bf16[32,16,128]{2,1,0:T(8,128)(2,1)} %bitcast.38, f32[1,128]{1,0:T(1,128)} %get-tuple-element.28.cnt.row.own_counts), custom_call_target="tpu_custom_call" | custom-call | tf_op jit(solution)/shard_map/halo/pallas_call | solution.py:53
  42.4 12.5 %hop.1 = bf16[16,128,128]{2,1,0:T(8,128)(2,1)} custom-call(s32[16,12]{1,0:T(8,128)} %lcols.1, s32[16,4]{1,0:T(8,128)} %copy.23.hcols, bf16[16,12,128,128]{3,2,1,0:T(8,128)(2,1)} %adj_l.1, bf16[16,4,128,128]{3,2,1,0:T(8,128)(2,1)} %adj_h.1, bf16[3,16,128,128]{3,2,1,0:T(8,128)(2,1)} %bitcast.36, bf16[4,128,128]{2,1,0:T(8,128)(2,1)} %bitcast.39), custom_call_target="tpu_custom_call" | custom-call | flops 1073741824 | bytes 9437184 | tf_op jit(solution)/shard_map/hop/pallas_call | solution.py:396
  54.9 0.1 broadcast_in_dim.32
  55.1 0.9 slice.17
  56.0 1.1 slice.16
  57.0 10.8 %pre.1 = (bf16[2048,512]{1,0:T(8,128)(2,1)}, f32[2048,1024]{1,0:T(8,128)}, f32[32,16,128]{2,1,0:T(8,128)}) custom-call(bf16[2048,384]{1,0:T(8,128)(2,1)} %get-tuple-element.30.x3, f32[2048,128]{1,0:T(8,128)} %get-tuple-element.31.tag, bf16[2048,128]{1,0:T(8,128)(2,1)} %bitcast.34, bf16[4,512,256]{2,1,0:T(8,128)(2,1)} %bitcast.33), custom_call_target="tpu_custom_call" | custom-call | tf_op jit(solution)/shard_map/pre/pallas_call | solution.py:414
  67.8 22.4 %stats_f.1 = (f32[32,16,128]{2,1,0:T(8,128)}, f32[1,128]{1,0:T(1,128)}) custom-call(f32[32,16,128]{2,1,0:T(8,128)} %get-tuple-element.36.src, f32[1,128]{1,0:T(1,128)} %get-tuple-element.28.cnt.row.own_counts), custom_call_target="tpu_custom_call" | custom-call | tf_op jit(solution)/shard_map/stats_f/pallas_call | solution.py:53
  90.2 13.6 %head.1 = (bf16[2048,172]{1,0:T(8,128)(2,1)}, f32[1024,172]{1,0:T(8,128)}, f32[32,16,128]{2,1,0:T(8,128)}, f32[1,128]{1,0:T(1,128)}) custom-call(f32[2048,1024]{1,0:T(8,128)} %get-tuple-element.35.z_ref, f32[2048,128]{1,0:T(8,128)} %get-tuple-element.31.tag, f32[32,16,128]{2,1,0:T(8,128)} %get-tuple-element.37.st, f32[1,128]{1,0:T(1,128)} %get-tuple-element.38.counts, ...), custom_call_target="tpu_custom_call" | custom-call | tf_op jit(solution)/shard_map/head/pallas_call | solution.py:437
  103.7 22.9 %stats_b.1 = (f32[32,16,128]{2,1,0:T(8,128)}, f32[1,128]{1,0:T(1,128)}) custom-call(f32[32,16,128]{2,1,0:T(8,128)} %get-tuple-element.39.src, f32[1,128]{1,0:T(1,128)} %get-tuple-element.40.row), custom_call_target="tpu_custom_call" | custom-call | tf_op jit(solution)/shard_map/stats_b/pallas_call | solution.py:53
  126.7 12.3 %tail.1.src = bf16[2,4,4,96,256]{4,3,2,1,0:T(8,128)(2,1)} custom-call(f32[2048,1024]{1,0:T(8,128)} %get-tuple-element.35.z_ref, bf16[2048,512]{1,0:T(8,128)(2,1)} %get-tuple-element.42.x_ref, f32[32,16,128]{2,1,0:T(8,128)} %get-tuple-element.37.st, f32[32,16,128]{2,1,0:T(8,128)} %get-tuple-element.43.gm, bf16[1024,172]{1,0:T(8,128)(2,1)} %bitcast.32, ...), custom_call_target="tpu_custom_call" | custom-call | tf_op jit(solution)/shard_map/tail/pallas_call | solution.py:454
  138.9 27.9 %grads.1 = (f32[64,256]{1,0:T(8,128)}, f32[8,32,256]{2,1,0:T(8,128)}) custom-call(bf16[2,4,4,96,256]{4,3,2,1,0:T(8,128)(2,1)} %tail.1.src), custom_call_target="tpu_custom_call" | custom-call | tf_op jit(solution)/shard_map/grads/pallas_call | solution.py:53
  166.8 1.7 %copy.26 = f32[256,172]{0,1:T(8,128)} copy(f32[256,172]{1,0:T(8,128)} %bitcast.37) | data formatting | bytes 352256
  168.6 0.5 copy.36
  169.1 1.5 copy.37
  (19 shorter events, 0.3 us)
Async XLA Ops:
  0.6 1.0 copy-start
  1.7 26.4 %collective-permute-start.2 = (bf16[384,256]{1,0:T(8,128)(2,1)S(1)}, bf16[384,256]{1,0:T(8,128)(2,1)S(1)}, u32[]{:S(2)}, u32[]{:S(2)}) collective-permute-start(bf16[384,256]{1,0:T(8,128)(2,1)S(1)} %fusion.1), channel_id=1, source_target_pairs={{0,3},{1,0},{2,1},{3,2},{4,7},{5,4},{6,5},{7,6},{8,11},{9,8},{10,9... | collective-permute-start | bytes 589832 | tf_op jit(solution)/shard_map/ppermute | solution.py:330
  6.8 21.2 %collective-permute-start.1 = (bf16[384,256]{1,0:T(8,128)(2,1)S(1)}, bf16[384,256]{1,0:T(8,128)(2,1)S(1)}, u32[]{:S(2)}, u32[]{:S(2)}) collective-permute-start(bf16[384,256]{1,0:T(8,128)(2,1)S(1)} %fusion.1), channel_id=1, source_target_pairs={{0,2},{1,3},{2,0},{3,1},{4,6},{5,7},{6,4},{7,5},{8,10},{9,11},{10,... | collective-permute-start | bytes 589832 | tf_op jit(solution)/shard_map/ppermute | solution.py:330
  6.8 21.2 %collective-permute-start = (bf16[384,256]{1,0:T(8,128)(2,1)S(1)}, bf16[384,256]{1,0:T(8,128)(2,1)S(1)}, u32[]{:S(2)}, u32[]{:S(2)}) collective-permute-start(bf16[384,256]{1,0:T(8,128)(2,1)S(1)} %fusion.1), channel_id=1, source_target_pairs={{0,1},{1,2},{2,3},{3,0},{4,5},{5,6},{6,7},{7,4},{8,9},{9,10},{10,1... | collective-permute-start | bytes 589832 | tf_op jit(solution)/shard_map/ppermute | solution.py:330
  27.9 0.7 copy-start.1
  28.1 26.9 %collective-permute-start.3 = (bf16[4,384,256]{2,1,0:T(8,128)(2,1)S(1)}, bf16[4,384,256]{2,1,0:T(8,128)(2,1)S(1)}, u32[]{:S(2)}, u32[]{:S(2)}) collective-permute-start(bf16[4,384,256]{2,1,0:T(8,128)(2,1)S(1)} %bitcast_dynamic-update-slice_fusion.2), channel_id=1, source_target_pairs={{0,4},{4,0},{8,12},{12,8},{16,20},{20,16},{24,28},{28,24},{1,5},{5... | collective-permute-start | bytes 2359304 | tf_op jit(solution)/shard_map/ppermute | solution.py:340
  138.9 29.6 %copy-start.2 = (f32[1,128]{1,0:T(1,128)S(1)}, f32[1,128]{1,0:T(1,128)}, u32[]{:S(2)}) copy-start(f32[1,128]{1,0:T(1,128)} %get-tuple-element.41) | copy-start | bytes 1540
where the time goes:
time: 172 us; the launch traced here: 171 us
  Pallas kernels  152 us (88%)
  local copies, waits for them, and re-layouts  11.5 us (7%)
  starting transfers between devices  6.21 us (4%)
    pallas_call x4, Pallas kernels, comm_call(): pl.pallas_call(kernel, out_shape=outs, in_specs=[pl.BlockSpec(memory_spac...  86.3 us
    pallas_call x1, Pallas kernels, shards(): pl.pallas_call(functools.partial(pick_kernel, chunk), out_shape=(sds((slo...  16.5 us
    pallas_call x1, Pallas kernels, shards(): pl.pallas_call(functools.partial(head_kernel, chunk), out_shape=(sds((slo...  13.6 us
    pallas_call x1, Pallas kernels, shards(): pl.pallas_call(functools.partial(hop_kernel, kl, kh), out_shape=sds((row_...  12.5 us
    pallas_call x1, Pallas kernels, shards(): pl.pallas_call(functools.partial(tail_kernel, chunk, ndom, nrep, cores),...  12.3 us
    pallas_call x1, Pallas kernels, shards(): pl.pallas_call(functools.partial(pre_kernel, chunk), out_shape=(sds((slot...  10.8 us
    ppermute x3, starting transfers between devices, send_rep(): lax.ppermute(half, 'rep', [(s, (s + o) % nrep) for s in range(nrep)])  6.14 us
    unnamed x11, local copies, waits for them, and re-layouts  4.88 us
  transfers between devices with their start and end apart: 4, of which 0 were waited for; matrix products, arithmetic and copies ran while one was open for 3% of the time, Pallas kernels for 25%

commit v1 on v0

v1 whole, which is shorter than its diff:
```python
import functools

import jax
import jax.numpy as jnp
from jax import lax
from jax.experimental import pallas as pl
from jax.experimental.pallas import tpu as pltpu
from jax.sharding import PartitionSpec as P

F32 = jnp.float32
BF16 = jnp.bfloat16
BIG = 60 * 1024 * 1024


def where_am_i(ndom, nrep):
    return lax.axis_index("dom") * nrep + lax.axis_index("rep")


def enter(me, n, nrep):
    barrier = pltpu.get_barrier_semaphore()

    def greet(o, carry):
        peer = lax.rem(me + o, n)
        pl.semaphore_signal(barrier, inc=1, device_id=(peer // nrep, lax.rem(peer, nrep)),
                            device_id_type=pl.DeviceIdType.MESH)
        return carry

    lax.fori_loop(1, n, greet, 0)
    pl.semaphore_wait(barrier, n - 1)


def spread(me, n, nrep, src_at, dst, send_sem, recv_sem):
    def copy(o):
        peer = lax.rem(me + o, n)
        return pltpu.make_async_remote_copy(
            src_ref=src_at(peer), dst_ref=dst.at[me],
            send_sem=send_sem.at[o], recv_sem=recv_sem.at[o],
            device_id=(peer // nrep, lax.rem(peer, nrep)),
            device_id_type=pl.DeviceIdType.MESH)

    def start(o, carry):
        copy(o).start()
        return carry

    def finish(o, carry):
        copy(o).wait()
        return carry

    return (lambda: lax.fori_loop(1, n, start, 0)), (lambda: lax.fori_loop(1, n, finish, 0))


def comm_call(kernel, outs, scratch, name, cid, *args):
    return pl.pallas_call(
        kernel,
        out_shape=outs,
        in_specs=[pl.BlockSpec(memory_space=pltpu.VMEM)] * len(args),
        out_specs=jax.tree.map(lambda _: pl.BlockSpec(memory_space=pltpu.VMEM), outs),
        scratch_shapes=scratch,
        compiler_params=pltpu.CompilerParams(collective_id=cid, has_side_effects=True),
        name=name,
    )(*args)


def dma_sems(n, count):
    return [pltpu.SemaphoreType.DMA((n,))] * count


def halo_kernel(ndom, nrep, src, cnt, out, tot, buf, crow, cbuf, ssem, rsem, s2, r2):
    n = ndom * nrep
    me = where_am_i(ndom, nrep)
    crow[0] = cnt[...]
    enter(me, n, nrep)
    start, finish = spread(me, n, nrep, lambda p: src.at[p], buf, ssem, rsem)
    cstart, cfinish = spread(me, n, nrep, lambda p: crow.at[0], cbuf, s2, r2)
    start()
    cstart()
    buf[me] = src[me]
    cbuf[me] = cnt[...]
    finish()
    cfinish()
    out[...] = buf[...]
    tot[...] = jnp.maximum(jnp.sum(cbuf[...], axis=0), 1.0)


def mlp_kernel(chunk, ndom, nrep, cores, classes, x3, tag, hop, w1, w2, counts, own_counts,
               first_out, second_out, loss_out,
               xs, xt, zs, gs, dzs, g2acc, acc, lrow, lbuf,
               fsrc, fin, fpart, fall, fgath, bsrc, bin_, bpart, ball, bgath,
               gsrc, gin, gsum, gnear, gfar, gkeep, gfarin,
               hsrc, hin, hsum, hnear, hkeep, hfar, hfarin, hgath,
               fx_s, fx_r, fa_s, fa_r, fg_s, fg_r, fw_s, fw_r,
               bx_s, bx_r, ba_s, ba_r, bg_s, bg_r, bw_s, bw_r,
               l_s, l_r, gx_s, gx_r, gn_s, gn_r, gf_s, gf_r,
               hx_s, hx_r, hn_s, hn_r, hf_s, hf_r, hg_s, hg_r):
    n = ndom * nrep
    chips = ndom // cores
    peers = chips * nrep
    dom, rep = lax.axis_index("dom"), lax.axis_index("rep")
    me = dom * nrep + rep
    chip, core = dom // cores, lax.rem(dom, cores)
    other = cores - 1 - core
    block = 256
    slots, hidden_units = zs.shape
    steps = slots // block
    groups = block // chunk
    half = fsrc.shape[1] // 2
    width = hidden_units // nrep
    per = half // nrep

    barrier = pltpu.get_barrier_semaphore()

    def greet(o, carry):
        peer = lax.rem(me + o, n)
        pl.semaphore_signal(barrier, inc=1, device_id=(peer // nrep, lax.rem(peer, nrep)),
                            device_id_type=pl.DeviceIdType.MESH)
        return carry

    lax.fori_loop(1, n, greet, 0)

    def to(src, dst, ssem, rsem, peer_dom, peer_rep):
        return pltpu.make_async_remote_copy(
            src_ref=src, dst_ref=dst, send_sem=ssem, recv_sem=rsem,
            device_id=(peer_dom, peer_rep), device_id_type=pl.DeviceIdType.MESH)

    def each(count, fn, first=0):
        lax.fori_loop(first, count, lambda i, carry: (fn(i), carry)[1], 0)

    def group_of(a, c):
        return pl.ds((a * cores + c) * nrep, nrep)

    def pre(i):
        at = pl.ds(pl.multiple_of(i * block, block), block)
        order = tag[at, 8:9].astype(jnp.int32)
        got = jnp.dot(one_hot(order, hop.shape[0]), hop[...], preferred_element_type=F32)
        x = jnp.concatenate([x3[at, :], got.astype(BF16)], axis=1)
        xs[at, :] = x
        here = pl.ds(i * groups, groups)
        for r in range(nrep):
            z = jnp.dot(x, w1[r], preferred_element_type=F32)
            zs[at, r * width:(r + 1) * width] = z
            z3 = z.reshape(groups, chunk, width)
            mean = jnp.sum(z3, axis=1, keepdims=True) * (1.0 / chunk)
            off = z3 - mean
            spread2 = jnp.sum(off * off, axis=1, keepdims=True)
            for j in range(per):
                cut = slice(j * 128, (j + 1) * 128)
                fsrc[here, r * per + j:r * per + j + 1] = mean[:, :, cut]
                fsrc[here, half + r * per + j:half + r * per + j + 1] = spread2[:, :, cut]

    each(steps, pre)
    pl.semaphore_wait(barrier, n - 1)

    def chip_sum(src, got, part, xs_, xr, combine):
        def swap(a):
            return to(src.at[group_of(a, other)], got.at[a], xs_.at[a], xr.at[a],
                      chip * cores + other, rep)

        def start():
            each(chips, lambda a: swap(a).start())

        def finish():
            def one(a):
                swap(a).wait()
                part[a] = combine(src[group_of(a, core)], got[a])
            each(chips, one)
        return start, finish

    def walk(o):
        return lax.rem(chip + o // nrep, chips), lax.rem(rep + lax.rem(o, nrep), nrep)

    def scatter(part, arrived, as_, ar):
        def copy(o):
            a, r = walk(o)
            return to(part.at[a, r], arrived.at[o], as_.at[o], ar.at[o], a * cores + core, r)

        def start():
            each(peers, lambda o: copy(o).start(), 1)
            arrived[0] = part[chip, rep]

        def finish():
            each(peers, lambda o: copy(o).wait(), 1)
        return start, finish

    def gather(gath, gs_, gr, ws, wr):
        def copy(o):
            a, r = walk(o)
            return to(gath.at[me], gath.at[me], gs_.at[o], gr.at[o], a * cores + core, r)

        def forward(da):
            at = group_of(lax.rem(chip + chips - da, chips), core)
            return to(gath.at[at], gath.at[at], ws.at[da], wr.at[da], chip * cores + other, rep)

        def start():
            each(peers, lambda o: copy(o).start(), 1)

        def finish():
            each(nrep, lambda o: copy(o).wait_recv(), 1)
            forward(0).start()

            def chip_in(da):
                each((da + 1) * nrep, lambda o: copy(o).wait_recv(), da * nrep)
                forward(da).start()
            each(chips, chip_in, 1)
            each(chips, lambda da: forward(da).wait())
            each(peers, lambda o: copy(o).wait_send(), 1)
        return start, finish

    def both_moments(a, b):
        ma, mb = a[:, :half], b[:, :half]
        gap = ma - mb
        spread2 = a[:, half:] + b[:, half:] + (0.5 * chunk) * gap * gap
        return jnp.concatenate([(ma + mb) * 0.5, spread2], axis=1)

    start, finish = chip_sum(fsrc, fin, fpart, fx_s, fx_r, both_moments)
    start()
    each(steps, lambda i: xt.__setitem__(
        (slice(None), pl.ds(pl.multiple_of(i * block, block), block)),
        xs[pl.ds(pl.multiple_of(i * block, block), block), :].T))
    finish()
    start, finish = scatter(fpart, fall, fa_s, fa_r)
    start()
    finish()
    got = fall[...]
    mu = jnp.sum(got[:, :half], axis=0) * (1.0 / peers)
    off = got[:, :half] - mu[None]
    m2 = jnp.sum(got[:, half:], axis=0) + (cores * chunk) * jnp.sum(off * off, axis=0)
    fgath[me] = jnp.concatenate([mu, lax.rsqrt(m2 * (1.0 / (n * chunk)) + 1e-05)], axis=0)
    start, finish = gather(fgath, fg_s, fg_r, fw_s, fw_r)
    start()
    g2acc[...] = jnp.zeros_like(g2acc)
    loss_row = jnp.zeros((1, lrow.shape[2]), F32)
    finish()

    second = w2[...]

    def head(i, loss_row):
        at = pl.ds(pl.multiple_of(i * block, block), block)
        here = pl.ds(i * groups, groups)
        z3 = zs[at, :].reshape(groups, chunk, hidden_units)
        st = fgath[here]
        mean = jnp.concatenate([st[:, j:j + 1] for j in range(half)], axis=2)
        rstd = jnp.concatenate([st[:, half + j:half + j + 1] for j in range(half)], axis=2)
        normed = ((z3 - mean) * rstd).reshape(block, hidden_units)
        zs[at, :] = normed
        hidden = jnp.maximum(normed, 0.0).astype(BF16)
        logits = jnp.dot(hidden, second, preferred_element_type=F32)
        lane = lax.broadcasted_iota(jnp.int32, logits.shape, 1)
        logits = jnp.where(lane < classes, logits, -1e30)
        row_max = jnp.max(logits, axis=1, keepdims=True)
        expos = jnp.exp(logits - row_max)
        totals = jnp.sum(expos, axis=1, keepdims=True)
        target = tag[at, 0:1].astype(jnp.int32)
        mark = tag[at, 1:2]
        onehot = (lane == target).astype(F32)
        cross = jnp.log(totals) + row_max - jnp.sum(onehot * logits, axis=1, keepdims=True)
        rows_at = i * block + lax.broadcasted_iota(jnp.int32, (block, counts.shape[1]), 0)
        mine = rows_at // chunk == lax.broadcasted_iota(jnp.int32, (block, counts.shape[1]), 1)
        count = jnp.sum(jnp.where(mine, counts[...], 0.0), axis=1, keepdims=True)
        dlogits = ((expos / totals - onehot) * (mark / count)).astype(BF16)
        g2acc[...] += lax.dot_general(hidden, dlogits, (((0,), (0,)), ((), ())), preferred_element_type=F32)
        masked = jnp.where(normed > 0, by_lanes(dlogits, second), 0.0)
        gs[at, :] = masked
        sums = jnp.sum(masked.reshape(groups, chunk, hidden_units), axis=1, keepdims=True)
        projs = jnp.sum((masked * normed).reshape(groups, chunk, hidden_units), axis=1, keepdims=True)
        for j in range(half):
            cut = slice(j * 128, (j + 1) * 128)
            bsrc[here, j:j + 1] = sums[:, :, cut]
            bsrc[here, half + j:half + j + 1] = projs[:, :, cut]
        return loss_row + jnp.sum(jnp.where(mine, mark * cross, 0.0), axis=0, keepdims=True)

    loss_row = lax.fori_loop(0, steps, head, loss_row)
    start, finish = chip_sum(bsrc, bin_, bpart, bx_s, bx_r, lambda a, b: a + b)
    start()
    loss_row = loss_row / jnp.maximum(own_counts[...], 1.0)
    lrow[0] = loss_row
    lbuf[me] = loss_row

    def send_loss(o):
        peer = lax.rem(me + o, n)
        return to(lrow.at[0], lbuf.at[me], l_s.at[o], l_r.at[o], peer // nrep, lax.rem(peer, nrep))

    part = hsrc.shape[3]
    for r in range(nrep):
        for d in range(ndom):
            first_row = (r * ndom + d) * part
            hsrc[d % cores, d // cores, r] = g2acc[first_row:first_row + part, :].astype(BF16)
    h_swap = to(hsrc.at[other], hin, hx_s.at[0], hx_r.at[0], chip * cores + other, rep)
    h_swap.start()
    finish()
    start, finish = scatter(bpart, ball, ba_s, ba_r)
    start()
    h_swap.wait()
    hsum[...] = (hsrc[core].astype(F32) + hin[...].astype(F32)).astype(BF16)
    finish()
    bgath[me] = jnp.sum(ball[...], axis=0) * (1.0 / (n * chunk))
    start, finish = gather(bgath, bg_s, bg_r, bw_s, bw_r)
    start()
    each(n, lambda o: send_loss(o).start(), 1)
    finish()

    def plane(o):
        return lax.rem(chip + o, chips)

    def h_near(o):
        return to(hsum.at[plane(o)], hnear.at[o - 1], hn_s.at[o], hn_r.at[o], plane(o) * cores + core, rep)

    def h_along(o):
        peer = lax.rem(rep + o, nrep)
        return to(hfar.at[peer], hfarin.at[o - 1], hf_s.at[o], hf_r.at[o], dom, peer)

    def h_round(o):
        return to(hgath.at[dom], hgath.at[dom], hg_s.at[o], hg_r.at[o], lax.rem(dom + o, ndom), rep)

    def h_stage(stage):
        if stage == 0:
            each(chips, lambda o: h_near(o).start(), 1)
        elif stage == 1:
            each(chips, lambda o: h_near(o).wait(), 1)
            total = hsrc[core, chip].astype(F32) + hin[chip].astype(F32)
            for o in range(1, chips):
                total = total + hnear[o - 1].astype(F32)
            hkeep[...] = total
            hfar[...] = total.astype(BF16)
            each(nrep, lambda o: h_along(o).start(), 1)
        elif stage == 2:
            each(nrep, lambda o: h_along(o).wait(), 1)
            total = hkeep[rep]
            for o in range(1, nrep):
                total = total + hfarin[o - 1].astype(F32)
            hgath[dom] = total
            each(ndom, lambda o: h_round(o).start(), 1)
        else:
            each(ndom, lambda o: h_round(o).wait(), 1)
            for d in range(ndom):
                second_out[d * part:(d + 1) * part, :] = hgath[d][:, :classes]

    high = acc.shape[0] // ndom

    def g_swap(r):
        return to(gsrc.at[r, other], gin.at[r], gx_s.at[r], gx_r.at[r], chip * cores + other, rep)

    def g_near(r, o):
        return to(gsum.at[r, plane(o)], gnear.at[r, o - 1], gn_s.at[r, o], gn_r.at[r, o],
                  plane(o) * cores + core, rep)

    def g_far(r):
        o = lax.rem(r - rep + nrep, nrep)
        return to(gfar.at[r], gfarin.at[o], gf_s.at[o], gf_r.at[o], dom, r)

    def g_stage(r, stage):
        if stage == 0:
            g_swap(r).start()
        elif stage == 1:
            g_swap(r).wait()
            gsum[r] = (gsrc[r, core].astype(F32) + gin[r].astype(F32)).astype(BF16)
            each(chips, lambda o: g_near(r, o).start(), 1)
        else:
            each(chips, lambda o: g_near(r, o).wait(), 1)
            total = gsrc[r, core, chip].astype(F32) + gin[r, chip].astype(F32)
            for o in range(1, chips):
                total = total + gnear[r, o - 1].astype(F32)
            gkeep[r] = total
            gfar[r] = total.astype(BF16)

            @pl.when(rep != r)
            def _():
                g_far(r).start()

    def tail(r):
        cols = slice(r * width, (r + 1) * width)

        def block_dz(i):
            at = pl.ds(pl.multiple_of(i * block, block), block)
            here = pl.ds(i * groups, groups)
            low = r * per

            def lines(ref, first):
                return jnp.concatenate(
                    [ref[here, first + j:first + j + 1] for j in range(per)], axis=2)

            masked = gs[at, cols].reshape(groups, chunk, width)
            normed = zs[at, cols].reshape(groups, chunk, width)
            dz = (masked - lines(bgath, low) - normed * lines(bgath, half + low)) * lines(fgath, half + low)
            dzs[at, :] = dz.reshape(block, width).astype(BF16)

        each(steps, block_dz)
        acc[...] = jnp.dot(xt[...], dzs[...], preferred_element_type=F32)
        for d in range(ndom):
            gsrc[r, d % cores, d // cores] = acc[d * high:(d + 1) * high, :].astype(BF16)

    for r in range(nrep):
        h_stage(r) if r < 4 else None
        tail(r)
        g_stage(r, 0)
        if r >= 1:
            g_stage(r - 1, 1)
        if r >= 2:
            g_stage(r - 2, 2)
    for s in range(nrep, 4):
        h_stage(s)
    g_stage(nrep - 1, 1)
    if nrep >= 2:
        g_stage(nrep - 2, 2)
    each(n, lambda o: send_loss(o).wait(), 1)
    losses = lbuf[...]
    source = lax.broadcasted_iota(jnp.int32, losses.shape, 0)
    lane = lax.broadcasted_iota(jnp.int32, losses.shape, 2)
    mine = jnp.sum(jnp.where(lane == me, losses, 0.0), axis=2, keepdims=True)
    loss_out[...] = jnp.sum(jnp.where(lane == source, mine, 0.0), axis=0)
    g_stage(nrep - 1, 2)

    def g_own(o):
        return to(gfar.at[rep], gfarin.at[o], gf_s.at[o], gf_r.at[o], dom, lax.rem(rep + o, nrep))

    each(nrep, lambda o: g_own(o).wait_recv(), 1)
    total = gkeep[rep]
    for o in range(1, nrep):
        total = total + gfarin[o].astype(F32)
    first_out[...] = total
    each(nrep, lambda o: g_own(o).wait_send(), 1)


def hop_kernel(kl, kh, lcols, hcols, adj_l, adj_h, own, halo, out):
    i = pl.program_id(0)
    left = jnp.concatenate([adj_l[0, k] for k in range(kl)] + [adj_h[0, k] for k in range(kh)], axis=1)
    right = jnp.concatenate(
        [own[0, lcols[i, k]] for k in range(kl)] + [halo[hcols[i, k]] for k in range(kh)], axis=0)
    out[0] = jnp.dot(left, right, preferred_element_type=F32).astype(BF16)


def batch_lanes(rows, wide, chunk):
    at = pl.program_id(0) * rows + lax.broadcasted_iota(jnp.int32, (rows, wide), 0)
    return at // chunk == lax.broadcasted_iota(jnp.int32, (rows, wide), 1)


def one_hot(column, count):
    lanes = lax.broadcasted_iota(jnp.int32, (column.shape[0], count), 1)
    return (lanes == column).astype(F32).astype(BF16)


def by_lanes(left, right):
    return lax.dot_general(left, right, (((1,), (1,)), ((), ())), preferred_element_type=F32)


def pick_kernel(chunk, shuf, bound, ids, labels, labelled, feats, x_out, tag_out, sent_out, cnt_out):
    rows = shuf.shape[0]
    nodes = feats.shape[1]
    sent_out[...] = jnp.dot(one_hot(bound[...], nodes), feats[2], preferred_element_type=F32).astype(BF16)
    numbers = ids[...]
    blank = jnp.zeros((6, nodes), F32)
    table = jnp.concatenate(
        [(numbers // 256).astype(F32), (numbers % 256).astype(F32), jnp.zeros((6, ids.shape[1]), F32)], axis=0)
    two = by_lanes(one_hot(shuf[...], ids.shape[1]), table.astype(BF16))
    order = two[:, 0:1] * 256.0 + two[:, 1:2]
    pick = one_hot(order.astype(jnp.int32), nodes)
    whole = jnp.concatenate([feats[0], feats[1], feats[2]], axis=1)
    x_out[...] = jnp.dot(pick, whole, preferred_element_type=F32).astype(BF16)
    marks = jnp.concatenate([labels[...].astype(F32), labelled[...].astype(F32), blank], axis=0)
    tags = by_lanes(pick, marks.astype(BF16))
    tag_out[:, 0:8] = tags
    tag_out[:, 8:9] = order

    @pl.when(pl.program_id(0) == 0)
    def _():
        cnt_out[...] = jnp.zeros_like(cnt_out)

    here = batch_lanes(rows, cnt_out.shape[1], chunk)
    cnt_out[...] += jnp.sum(jnp.where(here, tags[:, 1:2], 0.0), axis=0, keepdims=True)


def whole_spec(shape):
    return pl.BlockSpec(tuple(shape), lambda i: (0,) * len(shape))


def lead_spec(shape):
    return pl.BlockSpec(tuple(shape), lambda i: (i,) + (0,) * (len(shape) - 1))


def send_rep(half, nrep):
    return [lax.ppermute(half, "rep", [(s, (s + o) % nrep) for s in range(nrep)]) for o in range(1, nrep)]


def gather_rep(half, arrived, ndom, nrep, cores):
    dom, rep = lax.axis_index("dom"), lax.axis_index("rep")
    core = lax.rem(dom, cores)
    slots = jnp.zeros((nrep,) + half.shape, half.dtype)
    slots = lax.dynamic_update_slice(slots, half[None], (rep, 0, 0))
    for o in range(1, nrep):
        slots = lax.dynamic_update_slice(slots, arrived[o - 1][None], (lax.rem(rep - o + nrep, nrep), 0, 0))
    theirs = lax.ppermute(slots, "dom", [(d, d + 1 - 2 * (d % 2)) for d in range(ndom)])
    both = jnp.zeros((cores,) + slots.shape, slots.dtype)
    both = lax.dynamic_update_slice(both, slots[None], (core, 0, 0, 0))
    return lax.dynamic_update_slice(both, theirs[None], (cores - 1 - core, 0, 0, 0))


def shards(hop_feats, adj_local, local_cols, adj_halo, halo_cols, boundary_rows, train_ids,
           shuffle, labels, labelled, w_first, w_second):
    ndom, nrep = lax.axis_size("dom"), lax.axis_size("rep")
    n = ndom * nrep
    cores = 2
    row_tiles, kl, tile, _ = adj_local.shape
    kh = adj_halo.shape[1]
    rows, width = hop_feats.shape[1:]
    slots = train_ids.shape[1]
    hidden_units, classes = w_second.shape[0] * nrep, w_second.shape[1]
    chunk = slots // n
    block = 256
    steps = slots // block
    groups = block // chunk
    wide = -(-n // 128) * 128
    big = pltpu.CompilerParams(vmem_limit_bytes=BIG)
    sds = jax.ShapeDtypeStruct

    core = lax.rem(lax.axis_index("dom"), cores)
    own_cols = hidden_units // nrep
    h1, h2 = w_first.shape[0] // cores, w_second.shape[0] // cores
    half = jnp.concatenate([
        lax.dynamic_slice(w_first, (core * h1, 0), (h1, own_cols)),
        jnp.pad(lax.dynamic_slice(w_second, (core * h2, 0), (h2, classes)),
                ((0, 0), (0, own_cols - classes)))], axis=0)
    arrived = send_rep(half, nrep)

    sent_block = boundary_rows.shape[1] // steps
    x3, tags, sent, own_counts = pl.pallas_call(
        functools.partial(pick_kernel, chunk),
        out_shape=(sds((slots, 3 * width), BF16), sds((slots, 128), F32),
                   sds((boundary_rows.shape[1], width), BF16), sds((1, wide), F32)),
        grid=(steps,),
        in_specs=[lead_spec((block, 1)), lead_spec((sent_block, 1)), whole_spec((1, slots)),
                  whole_spec((1, rows)), whole_spec((1, rows)), whole_spec(hop_feats.shape)],
        out_specs=(lead_spec((block, 3 * width)), lead_spec((block, 128)),
                   lead_spec((sent_block, width)), whole_spec((1, wide))),
        compiler_params=big, name="pick",
        cost_estimate=pl.CostEstimate(flops=2 * slots * rows * 5 * width, bytes_accessed=4 << 20, transcendentals=0),
    )(shuffle[0][:, None], boundary_rows[0][:, None], train_ids, labels[None], labelled[None], hop_feats)

    arrived, own_counts = lax.optimization_barrier((arrived, own_counts))
    both = gather_rep(half, arrived, ndom, nrep, cores)
    sent = sent.reshape(n, -1, width)
    halo, counts = comm_call(
        functools.partial(halo_kernel, ndom, nrep), (sds(sent.shape, BF16), sds((1, wide), F32)),
        [pltpu.VMEM(sent.shape, BF16), pltpu.VMEM((1, 1, wide), F32), pltpu.VMEM((n, 1, wide), F32)]
        + dma_sems(n, 4), "halo", 1, sent, own_counts)
    halo = halo.reshape(-1, tile, width)

    next_hop = pl.pallas_call(
        functools.partial(hop_kernel, kl, kh),
        out_shape=sds((row_tiles, tile, width), BF16),
        grid=(row_tiles,),
        in_specs=[
            pl.BlockSpec(memory_space=pltpu.SMEM), pl.BlockSpec(memory_space=pltpu.SMEM),
            lead_spec((1, kl, tile, tile)), lead_spec((1, kh, tile, tile)),
            pl.BlockSpec((1, row_tiles, tile, width), lambda i: (2, 0, 0, 0)), whole_spec(halo.shape)],
        out_specs=lead_spec((1, tile, width)),
        compiler_params=big, name="hop",
        cost_estimate=pl.CostEstimate(flops=2 * rows * width * tile * (kl + kh), bytes_accessed=9 << 20, transcendentals=0),
    )(local_cols, halo_cols, adj_local, adj_halo, hop_feats.reshape(3, row_tiles, tile, width), halo)
    next_hop = next_hop.reshape(rows, width)

    w1 = both[:, :, :h1].transpose(1, 0, 2, 3).reshape(nrep, cores * h1, own_cols)
    w2 = both[:, :, h1:].transpose(1, 0, 2, 3).reshape(hidden_units, own_cols)
    span = own_cols

    lines = 2 * hidden_units // 128
    chips = ndom // cores
    peers = chips * nrep
    own_rows, part = 4 * width // ndom, hidden_units // n
    vm = pltpu.VMEM

    def moment_scratch():
        return [vm((n, lines, 128), F32), vm((chips, nrep, lines, 128), F32), vm((chips, nrep, lines, 128), F32),
                vm((peers, lines, 128), F32), vm((n, lines, 128), F32)]

    grad_block = (own_rows, own_cols)
    half_block = (part, span)
    scratch = [
        vm((slots, 4 * width), BF16), vm((4 * width, slots), BF16), vm((slots, hidden_units), F32),
        vm((slots, hidden_units), F32), vm((slots, own_cols), BF16), vm((hidden_units, span), F32),
        vm((4 * width, own_cols), F32), vm((1, 1, wide), F32), vm((n, 1, wide), F32),
        *moment_scratch(), *moment_scratch(),
        vm((nrep, cores, chips) + grad_block, BF16), vm((nrep, chips) + grad_block, BF16),
        vm((nrep, chips) + grad_block, BF16), vm((nrep, chips - 1) + grad_block, BF16),
        vm((nrep,) + grad_block, BF16), vm((nrep,) + grad_block, F32), vm((nrep,) + grad_block, BF16),
        vm((cores, chips, nrep) + half_block, BF16), vm((chips, nrep) + half_block, BF16),
        vm((chips, nrep) + half_block, BF16), vm((chips - 1, nrep) + half_block, BF16),
        vm((nrep,) + half_block, F32), vm((nrep,) + half_block, BF16), vm((nrep - 1,) + half_block, BF16),
        vm((ndom,) + half_block, F32),
    ]
    moment_sems = dma_sems(chips, 2) + dma_sems(peers, 4) + dma_sems(chips, 2)
    scratch += moment_sems + moment_sems + dma_sems(n, 2) + dma_sems(nrep, 2)
    scratch += [pltpu.SemaphoreType.DMA((nrep, chips))] * 2 + dma_sems(nrep, 2)
    scratch += dma_sems(1, 2) + dma_sems(chips, 2) + dma_sems(nrep, 2) + dma_sems(ndom, 2)
    vmem = pl.BlockSpec(memory_space=pltpu.VMEM)
    first, second, turned = pl.pallas_call(
        functools.partial(mlp_kernel, chunk, ndom, nrep, cores, classes),
        out_shape=(sds((own_rows, own_cols), F32), sds((hidden_units // nrep, classes), F32),
                   sds((1, wide), F32)),
        in_specs=[vmem] * 7,
        out_specs=(vmem, vmem, vmem),
        scratch_shapes=scratch,
        compiler_params=pltpu.CompilerParams(collective_id=2, has_side_effects=True, vmem_limit_bytes=BIG),
        name="mlp",
    )(x3, tags, next_hop, w1, w2, counts, own_counts)
    loss = turned[:, :n]
    return (next_hop, loss, first, second)


def solution(mesh):
    both = ("dom", "rep")
    placed = (
        P(None, both, None), P(both, None, None, None), P(both, None), P(both, None, None, None),
        P(both, None), P(both, None), P(both, None), P(both, None), P(both), P(both),
        P(None, "rep"), P("rep", None),
    )
    return jax.shard_map(
        shards, mesh=mesh, in_specs=placed,
        out_specs=(P(both, None), P(both, None), P("dom", "rep"), P("rep", None)),
        check_vma=False,
    )
```

time: 172 us -> 131 us (0.76)
  Pallas kernels: 152 us -> 111 us
    pallas_call x4 -> x1, Pallas kernels: 86.3 us -> 12.1 us  [comm_call(): pl.pallas_call(kernel, out_shape=outs, in_specs=[pl.BlockSpec(memory_spac...]
    pallas_call x3 -> x1, Pallas kernels: 36.6 us -> 70.3 us  [shards(): pl.pallas_call(functools.partial(mlp_kernel, chunk, ndom, nrep, cores, cl...]
  transfers between devices with their start and end apart: 4 -> 4, of which waited for: 0 -> 0; matrix products, arithmetic and copies ran while one was open for 3% -> 3% of each run, Pallas kernels for 25% -> 31%
where the time goes in v1:
time: 131 us
  Pallas kernels  111 us (85%)
  local copies, waits for them, and re-layouts  11.5 us (9%)
  starting transfers between devices  7.11 us (5%)
    pallas_call x1, Pallas kernels, shards(): pl.pallas_call(functools.partial(mlp_kernel, chunk, ndom, nrep, cores, cl...  70.3 us
    pallas_call x1, Pallas kernels, shards(): pl.pallas_call(functools.partial(pick_kernel, chunk), out_shape=(sds((slo...  16.5 us
    pallas_call x1, Pallas kernels, shards(): pl.pallas_call(functools.partial(hop_kernel, kl, kh), out_shape=sds((row_...  12.5 us
    pallas_call x1, Pallas kernels, comm_call(): pl.pallas_call(kernel, out_shape=outs, in_specs=[pl.BlockSpec(memory_spac...  12.1 us
    ppermute x3, starting transfers between devices, send_rep(): lax.ppermute(half, 'rep', [(s, (s + o) % nrep) for s in range(nrep)])  7.04 us
    unnamed x11, local copies, waits for them, and re-layouts  5.48 us
  transfers between devices with their start and end apart: 4, of which 0 were waited for; matrix products, arithmetic and copies ran while one was open for 3% of the time, Pallas kernels for 31%

profile of v1, /device:TPU:0, one launch (start us, length us, event | category | flops | bytes accessed | tf_op | source)
XLA Modules:
  0.0 130.9 jit_solution(4761515258363618834)
XLA Ops:
  0.6 0.0 copy-start
  0.7 0.8 constant_dynamic-slice_fusion
  1.5 0.1 copy.26
  1.7 3.1 %collective-permute-start = (bf16[384,256]{1,0:T(8,128)(2,1)S(1)}, bf16[384,256]{1,0:T(8,128)(2,1)S(1)}, u32[]{:S(2)}, u32[]{:S(2)}) collective-permute-start(bf16[384,256]{1,0:T(8,128)(2,1)S(1)} %fusion.1), channel_id=1, source_target_pairs={{0,1},{1,2},{2,3},{3,0},{4,5},{5,6},{6,7},{7,4},{8,9},{9,10},{10,1... | collective-permute-start | bytes 589832 | tf_op jit(solution)/shard_map/ppermute | solution.py:480
  4.8 2.6 %collective-permute-start.1 = (bf16[384,256]{1,0:T(8,128)(2,1)S(1)}, bf16[384,256]{1,0:T(8,128)(2,1)S(1)}, u32[]{:S(2)}, u32[]{:S(2)}) collective-permute-start(bf16[384,256]{1,0:T(8,128)(2,1)S(1)} %fusion.1), channel_id=1, source_target_pairs={{0,2},{1,3},{2,0},{3,1},{4,6},{5,7},{6,4},{7,5},{8,10},{9,11},{10,... | collective-permute-start | bytes 589832 | tf_op jit(solution)/shard_map/ppermute | solution.py:480
  7.4 1.3 %collective-permute-start.2 = (bf16[384,256]{1,0:T(8,128)(2,1)S(1)}, bf16[384,256]{1,0:T(8,128)(2,1)S(1)}, u32[]{:S(2)}, u32[]{:S(2)}) collective-permute-start(bf16[384,256]{1,0:T(8,128)(2,1)S(1)} %fusion.1), channel_id=1, source_target_pairs={{0,3},{1,0},{2,1},{3,2},{4,7},{5,4},{6,5},{7,6},{8,11},{9,8},{10,9... | collective-permute-start | bytes 589832 | tf_op jit(solution)/shard_map/ppermute | solution.py:480
  8.7 2.1 %copy.20.shuf = s32[2048,1]{1,0:T(8,128)} copy(s32[2048,1]{0,1:T(1,128)} %bitcast.36) | data formatting | bytes 16384 | tf_op jit(solution)/shard_map/broadcast_in_dim;squeeze | solution.py:535
  10.8 0.9 copy.21.bound
  11.6 16.5 %pick.1 = (bf16[2048,384]{1,0:T(8,128)(2,1)}, f32[2048,128]{1,0:T(8,128)}, bf16[512,128]{1,0:T(8,128)(2,1)}, f32[1,128]{1,0:T(1,128)}) custom-call(s32[2048,1]{1,0:T(8,128)} %copy.20.shuf, s32[512,1]{1,0:T(8,128)} %copy.21.bound, s32[1,2048]{1,0:T(1,128)} %ids.1, s32[1,2048]{1,0:T(1,128)} %bitcast.38, s32[1,2048]{1,0:T(1,128)} %bitcast.39, ...), custom_call_target="tpu_custom_call" | custom-call | flops 5368709120 | bytes 4194304 | tf_op jit(solution)/shard_map/pick/pallas_call | solution.py:524
  28.2 0.1 broadcast_in_dim.33
  28.4 0.1 collective-permute-start.3
  28.5 0.4 copy-done.2
  28.8 0.7 copy.23.hcols
  29.5 12.1 %halo.1 = (bf16[32,16,128]{2,1,0:T(8,128)(2,1)}, f32[1,128]{1,0:T(1,128)}) custom-call(bf16[32,16,128]{2,1,0:T(8,128)(2,1)} %bitcast.34, f32[1,128]{1,0:T(1,128)} %get-tuple-element.19.cnt.own_counts), custom_call_target="tpu_custom_call" | custom-call | tf_op jit(solution)/shard_map/halo/pallas_call | solution.py:53
  41.6 12.5 %hop.1 = bf16[16,128,128]{2,1,0:T(8,128)(2,1)} custom-call(s32[16,12]{1,0:T(8,128)} %lcols.1, s32[16,4]{1,0:T(8,128)} %copy.23.hcols, bf16[16,12,128,128]{3,2,1,0:T(8,128)(2,1)} %adj_l.1, bf16[16,4,128,128]{3,2,1,0:T(8,128)(2,1)} %adj_h.1, bf16[3,16,128,128]{3,2,1,0:T(8,128)(2,1)} %bitcast.33, bf16[4,128,128]{2,1,0:T(8,128)(2,1)} %bitcast.35), custom_call_target="tpu_custom_call" | custom-call | flops 1073741824 | bytes 9437184 | tf_op jit(solution)/shard_map/hop/pallas_call | solution.py:546
  54.1 0.1 broadcast_in_dim.32
  54.2 0.1 bitcast_dynamic-update-slice_fusion
  54.3 0.1 bitcast_dynamic-update-slice_fusion.1
  54.4 1.1 slice.12
  55.4 0.8 slice.13
  56.2 70.3 %mlp.1 = (f32[64,256]{1,0:T(8,128)}, f32[256,172]{1,0:T(8,128)}, f32[1,128]{1,0:T(1,128)}) custom-call(bf16[2048,384]{1,0:T(8,128)(2,1)} %get-tuple-element.21.x3, f32[2048,128]{1,0:T(8,128)} %get-tuple-element.22.tag, bf16[2048,128]{1,0:T(8,128)(2,1)} %bitcast.31, bf16[4,512,256]{2,1,0:T(8,128)(2,1)} %bitcast.29, bf16[1024,256]{1,0:T(8,128)(2,1)} %bitcast.30, ...), custom_call_target="tpu_custom_call" | custom-call | tf_op jit(solution)/shard_map/mlp/pallas_call | solution.py:594
  126.5 1.7 %copy.25 = f32[256,172]{0,1:T(8,128)} copy(f32[256,172]{1,0:T(8,128)} %get-tuple-element.37) | data formatting | bytes 352256
  128.3 1.1 copy.35
  129.4 1.5 %copy.36 = f32[64,256]{1,0:T(8,128)} copy(f32[64,256]{1,0:T(8,128)} %get-tuple-element.44) | data formatting | bytes 131072
  (14 shorter events, 0.1 us)
Async XLA Ops:
  0.6 1.0 copy-start
  0.6 10.1 %copy-start.1 = (s32[1,512]{1,0:T(1,128)S(1)}, s32[1,512]{1,0:T(1,128)}, u32[]{:S(2)}) copy-start(s32[1,512]{1,0:T(1,128)} %param.17) | copy-start | bytes 6148
  1.7 26.6 %collective-permute-start = (bf16[384,256]{1,0:T(8,128)(2,1)S(1)}, bf16[384,256]{1,0:T(8,128)(2,1)S(1)}, u32[]{:S(2)}, u32[]{:S(2)}) collective-permute-start(bf16[384,256]{1,0:T(8,128)(2,1)S(1)} %fusion.1), channel_id=1, source_target_pairs={{0,1},{1,2},{2,3},{3,0},{4,5},{5,6},{6,7},{7,4},{8,9},{9,10},{10,1... | collective-permute-start | bytes 589832 | tf_op jit(solution)/shard_map/ppermute | solution.py:480
  4.8 23.5 %collective-permute-start.1 = (bf16[384,256]{1,0:T(8,128)(2,1)S(1)}, bf16[384,256]{1,0:T(8,128)(2,1)S(1)}, u32[]{:S(2)}, u32[]{:S(2)}) collective-permute-start(bf16[384,256]{1,0:T(8,128)(2,1)S(1)} %fusion.1), channel_id=1, source_target_pairs={{0,2},{1,3},{2,0},{3,1},{4,6},{5,7},{6,4},{7,5},{8,10},{9,11},{10,... | collective-permute-start | bytes 589832 | tf_op jit(solution)/shard_map/ppermute | solution.py:480
  7.4 20.9 %collective-permute-start.2 = (bf16[384,256]{1,0:T(8,128)(2,1)S(1)}, bf16[384,256]{1,0:T(8,128)(2,1)S(1)}, u32[]{:S(2)}, u32[]{:S(2)}) collective-permute-start(bf16[384,256]{1,0:T(8,128)(2,1)S(1)} %fusion.1), channel_id=1, source_target_pairs={{0,3},{1,0},{2,1},{3,2},{4,7},{5,4},{6,5},{7,6},{8,11},{9,8},{10,9... | collective-permute-start | bytes 589832 | tf_op jit(solution)/shard_map/ppermute | solution.py:480
  28.1 0.7 copy-start.2
  28.4 25.9 %collective-permute-start.3 = (bf16[4,384,256]{2,1,0:T(8,128)(2,1)S(1)}, bf16[4,384,256]{2,1,0:T(8,128)(2,1)S(1)}, u32[]{:S(2)}, u32[]{:S(2)}) collective-permute-start(bf16[4,384,256]{2,1,0:T(8,128)(2,1)S(1)} %bitcast_dynamic-update-slice_fusion.2), channel_id=1, source_target_pairs={{0,4},{4,0},{8,12},{12,8},{16,20},{20,16},{24,28},{28,24},{1,5},{5... | collective-permute-start | bytes 2359304 | tf_op jit(solution)/shard_map/ppermute | solution.py:490

commit v2 on v1

--- a/solution.py
+++ b/solution.py
@@ -9,81 +9,25 @@
 
 F32 = jnp.float32
 BF16 = jnp.bfloat16
-BIG = 60 * 1024 * 1024
-
-
-def where_am_i(ndom, nrep):
-    return lax.axis_index("dom") * nrep + lax.axis_index("rep")
-
-
-def enter(me, n, nrep):
-    barrier = pltpu.get_barrier_semaphore()
-
-    def greet(o, carry):
-        peer = lax.rem(me + o, n)
-        pl.semaphore_signal(barrier, inc=1, device_id=(peer // nrep, lax.rem(peer, nrep)),
-                            device_id_type=pl.DeviceIdType.MESH)
-        return carry
-
-    lax.fori_loop(1, n, greet, 0)
-    pl.semaphore_wait(barrier, n - 1)
-
-
-def spread(me, n, nrep, src_at, dst, send_sem, recv_sem):
-    def copy(o):
-        peer = lax.rem(me + o, n)
-        return pltpu.make_async_remote_copy(
-            src_ref=src_at(peer), dst_ref=dst.at[me],
-            send_sem=send_sem.at[o], recv_sem=recv_sem.at[o],
-            device_id=(peer // nrep, lax.rem(peer, nrep)),
-            device_id_type=pl.DeviceIdType.MESH)
-
-    def start(o, carry):
-        copy(o).start()
-        return carry
-
-    def finish(o, carry):
-        copy(o).wait()
-        return carry
-
-    return (lambda: lax.fori_loop(1, n, start, 0)), (lambda: lax.fori_loop(1, n, finish, 0))
-
-
-def comm_call(kernel, outs, scratch, name, cid, *args):
-    return pl.pallas_call(
-        kernel,
-        out_shape=outs,
-        in_specs=[pl.BlockSpec(memory_space=pltpu.VMEM)] * len(args),
-        out_specs=jax.tree.map(lambda _: pl.BlockSpec(memory_space=pltpu.VMEM), outs),
-        scratch_shapes=scratch,
-        compiler_params=pltpu.CompilerParams(collective_id=cid, has_side_effects=True),
-        name=name,
-    )(*args)
-
-
-def dma_sems(n, count):
-    return [pltpu.SemaphoreType.DMA((n,))] * count
-
-
-def halo_kernel(ndom, nrep, src, cnt, out, tot, buf, crow, cbuf, ssem, rsem, s2, r2):
-    n = ndom * nrep
-    me = where_am_i(ndom, nrep)
-    crow[0] = cnt[...]
-    enter(me, n, nrep)
-    start, finish = spread(me, n, nrep, lambda p: src.at[p], buf, ssem, rsem)
-    cstart, cfinish = spread(me, n, nrep, lambda p: crow.at[0], cbuf, s2, r2)
-    start()
-    cstart()
-    buf[me] = src[me]
-    cbuf[me] = cnt[...]
-    finish()
-    cfinish()
-    out[...] = buf[...]
-    tot[...] = jnp.maximum(jnp.sum(cbuf[...], axis=0), 1.0)
-
-
-def mlp_kernel(chunk, ndom, nrep, cores, classes, x3, tag, hop, w1, w2, counts, own_counts,
-               first_out, second_out, loss_out,
+BIG = 63 * 1024 * 1024
+LANES = 128
+
+
+def one_hot(column, count):
+    lanes = lax.broadcasted_iota(jnp.int32, (column.shape[0], count), 1)
+    return (lanes == column).astype(F32).astype(BF16)
+
+
+def by_lanes(left, right):
+    return lax.dot_general(left, right, (((1,), (1,)), ((), ())), preferred_element_type=F32)
+
+
+def step_kernel(chunk, ndom, nrep, cores, classes, kl, kh,
+               lcols, hcols, w1in, w2in, feats, adj_l, adj_h, tiles, bound, ids, shuf, labels, labelled,
+               next_out, first_out, second_out, loss_out,
+               ints, cols, order, whole, adjv, hacc, nh, pick, sent, halo, own_t, halo_t, tag, w1all, w2all, crow, cbuf,
+               f_s, t_s, a_s, b_s, i_s, c_s, c_r, p_s, p_r, uz_s, uz_r, up_s, up_r, uc_s, uc_r,
+               vz_s, vz_r, vp_s, vp_r, vc_s, vc_r,
                xs, xt, zs, gs, dzs, g2acc, acc, lrow, lbuf,
                fsrc, fin, fpart, fall, fgath, bsrc, bin_, bpart, ball, bgath,
                gsrc, gin, gsum, gnear, gfar, gkeep, gfarin,
@@ -128,15 +72,191 @@
     def group_of(a, c):
         return pl.ds((a * cores + c) * nrep, nrep)
 
+    def plane(o):
+        return lax.rem(chip + o, chips)
+
+    def rows_of(i):
+        return pl.ds(pl.multiple_of(i * block, block), block)
+
+    row_tiles, tile, fw = hacc.shape
+    nodes = whole.shape[0]
+
+    def feat_copy(k):
+        return pltpu.make_async_copy(feats.at[k], whole.at[:, k * fw:(k + 1) * fw], f_s.at[k])
+
+    def near_copy(i):
+        return pltpu.make_async_copy(adj_l.at[i], adjv.at[i, 0:kl], a_s.at[i])
+
+    def far_copy(i):
+        return pltpu.make_async_copy(adj_h.at[i], adjv.at[i, kl:kl + kh], b_s.at[i])
+
+    given = (shuf, ids, labels, labelled, bound)
+    int_copies = [pltpu.make_async_copy(ref, ints.at[m:m + 1, 0:ref.shape[1]], i_s.at[m])
+                  for m, ref in enumerate(given)]
+    for copy in int_copies:
+        copy.start()
+    own_copy = pltpu.make_async_copy(tiles.at[2], own_t, t_s.at[0])
+    own_copy.start()
+    feat_copy(2).start()
+    feat_copy(0).start()
+    feat_copy(1).start()
+    each(row_tiles, lambda i: near_copy(i).start())
+    each(row_tiles, lambda i: far_copy(i).start())
+
+    w1all[rep] = w1in[...].reshape(w1all.shape[1:])
+    w2pad = jnp.concatenate(
+        [w2in[...], jnp.zeros((w2in.shape[0], w2all.shape[3] - classes), BF16)], axis=1)
+    w2all[rep] = w2pad.reshape(w2all.shape[1:])
+    for copy in int_copies:
+        copy.wait()
+
+    def lines_of(m, count):
+        return jnp.concatenate([ints[m:m + 1, j * LANES:(j + 1) * LANES] for j in range(count)], axis=0)
+
+    per_slot, per_node, per_bound = slots // LANES, nodes // LANES, bound.shape[1] // LANES
+    shuf_lines, id_lines = lines_of(0, per_slot), lines_of(1, per_slot)
+    stack = [shuf_lines % LANES, shuf_lines // LANES, id_lines // LANES, id_lines % LANES,
+             lines_of(2, per_node), lines_of(3, per_node), lines_of(4, per_bound)]
+    used = sum(s.shape[0] for s in stack)
+    stack = jnp.concatenate(stack + [jnp.zeros((LANES - used, LANES), jnp.int32)], axis=0)
+    turned = stack.astype(F32).T
+    cols[...] = turned
+
+    def column(m):
+        return cols[:, m:m + 1]
+
+    at_bound = 2 * per_slot + 2 * per_slot + 2 * per_node
+    own_copy.wait()
+    last = own_t[...].reshape(nodes, fw)
+    share = sent.shape[1]
+    for m in range(per_bound):
+        spot = one_hot(column(at_bound + m).astype(jnp.int32), nodes)
+        rows = jnp.dot(spot, last, preferred_element_type=F32)
+        count = LANES // share
+        sent[m * count:(m + 1) * count] = rows.reshape(count, share, fw).astype(BF16)
+    pl.semaphore_wait(barrier, n - 1)
+
+    def send_halo(o):
+        peer = lax.rem(me + o, n)
+        return to(sent.at[peer], halo.at[me], p_s.at[o], p_r.at[o], peer // nrep, lax.rem(peer, nrep))
+
+    def spread_weights(buf, zsem, zrec, psem, prec, csem, crec):
+        def along(o):
+            return to(buf.at[rep, dom], buf.at[rep, dom], zsem.at[o], zrec.at[o], dom, lax.rem(rep + o, nrep))
+
+        def across(p, o):
+            at = lax.rem(rep + o, nrep)
+            return to(buf.at[at, dom], buf.at[at, dom], psem.at[p, o], prec.at[p, o],
+                      plane(p) * cores + core, rep)
+
+        def swap(p, o):
+            at = lax.rem(rep + o, nrep)
+            src = buf.at[at, lax.rem(chip - p + chips, chips) * cores + core]
+            return to(src, src, csem.at[p, o], crec.at[p, o], chip * cores + other, rep)
+
+        def each_pair(first, fn):
+            each(chips, lambda p: each(nrep, lambda o: fn(p, o), 1), first)
+
+        def stage(s):
+            if s == 0:
+                each(nrep, lambda o: along(o).start(), 1)
+            elif s == 1:
+                each(nrep, lambda o: along(o).wait(), 1)
+                each_pair(1, lambda p, o: across(p, o).start())
+                each(nrep, lambda o: swap(0, o).start(), 1)
+            elif s == 2:
+                each_pair(1, lambda p, o: across(p, o).wait())
+                each_pair(1, lambda p, o: swap(p, o).start())
+            else:
+                each_pair(0, lambda p, o: swap(p, o).wait())
+        return stage
+
+    w1_stage = spread_weights(w1all, uz_s, uz_r, up_s, up_r, uc_s, uc_r)
+    w2_stage = spread_weights(w2all, vz_s, vz_r, vp_s, vp_r, vc_s, vc_r)
+    each(n, lambda o: send_halo(o).start(), 1)
+    w1_stage(0)
+    w2_stage(0)
+    halo[me] = sent[me]
+
+    lane = lax.broadcasted_iota(jnp.int32, (LANES, LANES), 1).astype(F32)
+    table = cols[:, 2 * per_slot:4 * per_slot].astype(BF16)
+    pair = lax.broadcasted_iota(jnp.int32, (LANES, 2 * per_slot), 1).astype(F32)
+    for k in range(per_slot):
+        low = (lane == column(k)).astype(F32).astype(BF16)
+        found = jnp.dot(low, table, preferred_element_type=F32)
+        high = column(per_slot + k)
+        value = jnp.where(pair == high, found * LANES, jnp.where(pair == high + per_slot, found, 0.0))
+        order[k * LANES:(k + 1) * LANES, 0:1] = jnp.sum(value, axis=1, keepdims=True)
+    for k in range(per_node):
+        marks = jnp.where(lane == 0, column(4 * per_slot + k),
+                          jnp.where(lane == 1, column(4 * per_slot + per_node + k), 0.0))
+        whole[k * LANES:(k + 1) * LANES, 3 * fw:4 * fw] = marks.astype(BF16)
+    for k in range(3):
+        feat_copy(k).wait()
+
+    def batch_rows(i):
+        rows_at = i * block + lax.broadcasted_iota(jnp.int32, (block, crow.shape[2]), 0)
+        return rows_at // chunk == lax.broadcasted_iota(jnp.int32, (block, crow.shape[2]), 1)
+
+    def gather_rows(i, own):
+        at = rows_of(i)
+        spot = one_hot(order[at, 0:1].astype(jnp.int32), nodes)
+        pick[at, :] = spot
+        rows = jnp.dot(spot, whole[...], preferred_element_type=F32)
+        xs[at, 0:3 * fw] = rows[:, 0:3 * fw].astype(BF16)
+        tags = rows[:, 3 * fw:4 * fw]
+        tag[at, :] = tags
+        return own + jnp.sum(jnp.where(batch_rows(i), tags[:, 1:2], 0.0), axis=0, keepdims=True)
+
+    own_counts = lax.fori_loop(0, steps, gather_rows, jnp.zeros((1, crow.shape[2]), F32))
+    w1_stage(1)
+    w2_stage(1)
+    crow[0] = own_counts
+    cbuf[me] = own_counts
+
+    def send_count(o):
+        peer = lax.rem(me + o, n)
+        return to(crow.at[0], cbuf.at[me], c_s.at[o], c_r.at[o], peer // nrep, lax.rem(peer, nrep))
+
+    each(n, lambda o: send_count(o).start(), 1)
+
+    def hop_near(i):
+        near_copy(i).wait()
+        left = jnp.concatenate([adjv[i, k] for k in range(kl)], axis=1)
+        right = jnp.concatenate([own_t[lcols[i, k]] for k in range(kl)], axis=0)
+        hacc[i] = jnp.dot(left, right, preferred_element_type=F32)
+
+    each(row_tiles, hop_near)
+    each(n, lambda o: send_halo(o).wait(), 1)
+    halo_t[...] = halo[...].reshape(halo_t.shape)
+
+    def hop_far(i):
+        far_copy(i).wait()
+        left = jnp.concatenate([adjv[i, kl + k] for k in range(kh)], axis=1)
+        right = jnp.concatenate(
+            [halo_t[hcols[i, k]] for k in range(kh)], axis=0)
+        total = (hacc[i] + jnp.dot(left, right, preferred_element_type=F32)).astype(BF16)
+        nh[pl.ds(pl.multiple_of(i * tile, tile), tile), :] = total
+        next_out[pl.ds(pl.multiple_of(i * tile, tile), tile), :] = total
+
+    each(row_tiles, hop_far)
+    w1_stage(2)
+    w2_stage(2)
+
+    def gather_next(i):
+        at = rows_of(i)
+        xs[at, 3 * fw:4 * fw] = jnp.dot(pick[at, :], nh[...], preferred_element_type=F32).astype(BF16)
+
+    each(steps, gather_next)
+    w1_stage(3)
+
     def pre(i):
-        at = pl.ds(pl.multiple_of(i * block, block), block)
-        order = tag[at, 8:9].astype(jnp.int32)
-        got = jnp.dot(one_hot(order, hop.shape[0]), hop[...], preferred_element_type=F32)
-        x = jnp.concatenate([x3[at, :], got.astype(BF16)], axis=1)
-        xs[at, :] = x
+        at = rows_of(i)
         here = pl.ds(i * groups, groups)
+        x = xs[at, :]
         for r in range(nrep):
-            z = jnp.dot(x, w1[r], preferred_element_type=F32)
+            w1 = w1all[r].reshape(w1in.shape)
+            z = jnp.dot(x, w1, preferred_element_type=F32)
             zs[at, r * width:(r + 1) * width] = z
             z3 = z.reshape(groups, chunk, width)
             mean = jnp.sum(z3, axis=1, keepdims=True) * (1.0 / chunk)
@@ -148,7 +268,6 @@
                 fsrc[here, half + r * per + j:half + r * per + j + 1] = spread2[:, :, cut]
 
     each(steps, pre)
-    pl.semaphore_wait(barrier, n - 1)
 
     def chip_sum(src, got, part, xs_, xr, combine):
         def swap(a):
@@ -229,9 +348,12 @@
     start()
     g2acc[...] = jnp.zeros_like(g2acc)
     loss_row = jnp.zeros((1, lrow.shape[2]), F32)
+    w2_stage(3)
+    each(n, lambda o: send_count(o).wait(), 1)
+    counts = jnp.maximum(jnp.sum(cbuf[...], axis=0), 1.0)
     finish()
 
-    second = w2[...]
+    second = w2all[...].reshape(hidden_units, w2all.shape[3])
 
     def head(i, loss_row):
         at = pl.ds(pl.multiple_of(i * block, block), block)
@@ -253,9 +375,8 @@
         mark = tag[at, 1:2]
         onehot = (lane == target).astype(F32)
         cross = jnp.log(totals) + row_max - jnp.sum(onehot * logits, axis=1, keepdims=True)
-        rows_at = i * block + lax.broadcasted_iota(jnp.int32, (block, counts.shape[1]), 0)
-        mine = rows_at // chunk == lax.broadcasted_iota(jnp.int32, (block, counts.shape[1]), 1)
-        count = jnp.sum(jnp.where(mine, counts[...], 0.0), axis=1, keepdims=True)
+        mine = batch_rows(i)
+        count = jnp.sum(jnp.where(mine, counts, 0.0), axis=1, keepdims=True)
         dlogits = ((expos / totals - onehot) * (mark / count)).astype(BF16)
         g2acc[...] += lax.dot_general(hidden, dlogits, (((0,), (0,)), ((), ())), preferred_element_type=F32)
         masked = jnp.where(normed > 0, by_lanes(dlogits, second), 0.0)
@@ -271,7 +392,7 @@
     loss_row = lax.fori_loop(0, steps, head, loss_row)
     start, finish = chip_sum(bsrc, bin_, bpart, bx_s, bx_r, lambda a, b: a + b)
     start()
-    loss_row = loss_row / jnp.maximum(own_counts[...], 1.0)
+    loss_row = loss_row / jnp.maximum(own_counts, 1.0)
     lrow[0] = loss_row
     lbuf[me] = loss_row
 
@@ -297,9 +418,6 @@
     start()
     each(n, lambda o: send_loss(o).start(), 1)
     finish()
-
-    def plane(o):
-        return lax.rem(chip + o, chips)
 
     def h_near(o):
         return to(hsum.at[plane(o)], hnear.at[o - 1], hn_s.at[o], hn_r.at[o], plane(o) * cores + core, rep)
@@ -406,7 +524,7 @@
     source = lax.broadcasted_iota(jnp.int32, losses.shape, 0)
     lane = lax.broadcasted_iota(jnp.int32, losses.shape, 2)
     mine = jnp.sum(jnp.where(lane == me, losses, 0.0), axis=2, keepdims=True)
-    loss_out[...] = jnp.sum(jnp.where(lane == source, mine, 0.0), axis=0)
+    loss_out[...] = jnp.sum(jnp.where(lane == source, mine, 0.0), axis=0)[:, :n]
     g_stage(nrep - 1, 2)
 
     def g_own(o):
@@ -468,29 +586,8 @@
     cnt_out[...] += jnp.sum(jnp.where(here, tags[:, 1:2], 0.0), axis=0, keepdims=True)
 
 
-def whole_spec(shape):
-    return pl.BlockSpec(tuple(shape), lambda i: (0,) * len(shape))
-
-
-def lead_spec(shape):
-    return pl.BlockSpec(tuple(shape), lambda i: (i,) + (0,) * (len(shape) - 1))
-
-
-def send_rep(half, nrep):
-    return [lax.ppermute(half, "rep", [(s, (s + o) % nrep) for s in range(nrep)]) for o in range(1, nrep)]
-
-
-def gather_rep(half, arrived, ndom, nrep, cores):
-    dom, rep = lax.axis_index("dom"), lax.axis_index("rep")
-    core = lax.rem(dom, cores)
-    slots = jnp.zeros((nrep,) + half.shape, half.dtype)
-    slots = lax.dynamic_update_slice(slots, half[None], (rep, 0, 0))
-    for o in range(1, nrep):
-        slots = lax.dynamic_update_slice(slots, arrived[o - 1][None], (lax.rem(rep - o + nrep, nrep), 0, 0))
-    theirs = lax.ppermute(slots, "dom", [(d, d + 1 - 2 * (d % 2)) for d in range(ndom)])
-    both = jnp.zeros((cores,) + slots.shape, slots.dtype)
-    both = lax.dynamic_update_slice(both, slots[None], (core, 0, 0, 0))
-    return lax.dynamic_update_slice(both, theirs[None], (cores - 1 - core, 0, 0, 0))
+def dma_sems(n, count):
+    return [pltpu.SemaphoreType.DMA((n,))] * count
 
 
 def shards(hop_feats, adj_local, local_cols, adj_halo, halo_cols, boundary_rows, train_ids,
@@ -500,80 +597,44 @@
     cores = 2
     row_tiles, kl, tile, _ = adj_local.shape
     kh = adj_halo.shape[1]
-    rows, width = hop_feats.shape[1:]
+    nodes, width = hop_feats.shape[1:]
     slots = train_ids.shape[1]
     hidden_units, classes = w_second.shape[0] * nrep, w_second.shape[1]
     chunk = slots // n
-    block = 256
-    steps = slots // block
-    groups = block // chunk
-    wide = -(-n // 128) * 128
-    big = pltpu.CompilerParams(vmem_limit_bytes=BIG)
+    wide = -(-n // LANES) * LANES
     sds = jax.ShapeDtypeStruct
-
-    core = lax.rem(lax.axis_index("dom"), cores)
     own_cols = hidden_units // nrep
-    h1, h2 = w_first.shape[0] // cores, w_second.shape[0] // cores
-    half = jnp.concatenate([
-        lax.dynamic_slice(w_first, (core * h1, 0), (h1, own_cols)),
-        jnp.pad(lax.dynamic_slice(w_second, (core * h2, 0), (h2, classes)),
-                ((0, 0), (0, own_cols - classes)))], axis=0)
-    arrived = send_rep(half, nrep)
-
-    sent_block = boundary_rows.shape[1] // steps
-    x3, tags, sent, own_counts = pl.pallas_call(
-        functools.partial(pick_kernel, chunk),
-        out_shape=(sds((slots, 3 * width), BF16), sds((slots, 128), F32),
-                   sds((boundary_rows.shape[1], width), BF16), sds((1, wide), F32)),
-        grid=(steps,),
-        in_specs=[lead_spec((block, 1)), lead_spec((sent_block, 1)), whole_spec((1, slots)),
-                  whole_spec((1, rows)), whole_spec((1, rows)), whole_spec(hop_feats.shape)],
-        out_specs=(lead_spec((block, 3 * width)), lead_spec((block, 128)),
-                   lead_spec((sent_block, width)), whole_spec((1, wide))),
-        compiler_params=big, name="pick",
-        cost_estimate=pl.CostEstimate(flops=2 * slots * rows * 5 * width, bytes_accessed=4 << 20, transcendentals=0),
-    )(shuffle[0][:, None], boundary_rows[0][:, None], train_ids, labels[None], labelled[None], hop_feats)
-
-    arrived, own_counts = lax.optimization_barrier((arrived, own_counts))
-    both = gather_rep(half, arrived, ndom, nrep, cores)
-    sent = sent.reshape(n, -1, width)
-    halo, counts = comm_call(
-        functools.partial(halo_kernel, ndom, nrep), (sds(sent.shape, BF16), sds((1, wide), F32)),
-        [pltpu.VMEM(sent.shape, BF16), pltpu.VMEM((1, 1, wide), F32), pltpu.VMEM((n, 1, wide), F32)]
-        + dma_sems(n, 4), "halo", 1, sent, own_counts)
-    halo = halo.reshape(-1, tile, width)
-
-    next_hop = pl.pallas_call(
-        functools.partial(hop_kernel, kl, kh),
-        out_shape=sds((row_tiles, tile, width), BF16),
-        grid=(row_tiles,),
-        in_specs=[
-            pl.BlockSpec(memory_space=pltpu.SMEM), pl.BlockSpec(memory_space=pltpu.SMEM),
-            lead_spec((1, kl, tile, tile)), lead_spec((1, kh, tile, tile)),
-            pl.BlockSpec((1, row_tiles, tile, width), lambda i: (2, 0, 0, 0)), whole_spec(halo.shape)],
-        out_specs=lead_spec((1, tile, width)),
-        compiler_params=big, name="hop",
-        cost_estimate=pl.CostEstimate(flops=2 * rows * width * tile * (kl + kh), bytes_accessed=9 << 20, transcendentals=0),
-    )(local_cols, halo_cols, adj_local, adj_halo, hop_feats.reshape(3, row_tiles, tile, width), halo)
-    next_hop = next_hop.reshape(rows, width)
-
-    w1 = both[:, :, :h1].transpose(1, 0, 2, 3).reshape(nrep, cores * h1, own_cols)
-    w2 = both[:, :, h1:].transpose(1, 0, 2, 3).reshape(hidden_units, own_cols)
-    span = own_cols
-
-    lines = 2 * hidden_units // 128
+    span = -(-classes // LANES) * LANES
+    lines = 2 * hidden_units // LANES
     chips = ndom // cores
     peers = chips * nrep
     own_rows, part = 4 * width // ndom, hidden_units // n
+    share = boundary_rows.shape[1] // n
     vm = pltpu.VMEM
 
     def moment_scratch():
-        return [vm((n, lines, 128), F32), vm((chips, nrep, lines, 128), F32), vm((chips, nrep, lines, 128), F32),
-                vm((peers, lines, 128), F32), vm((n, lines, 128), F32)]
+        return [vm((n, lines, LANES), F32), vm((chips, nrep, lines, LANES), F32),
+                vm((chips, nrep, lines, LANES), F32), vm((peers, lines, LANES), F32), vm((n, lines, LANES), F32)]
+
+    def pairs(a, b, count):
+        return [pltpu.SemaphoreType.DMA((a, b))] * count
 
     grad_block = (own_rows, own_cols)
     half_block = (part, span)
     scratch = [
+        vm((8, max(slots, nodes)), jnp.int32), vm((LANES, LANES), F32), vm((slots, LANES), F32),
+        vm((nodes, 4 * width), BF16), vm((row_tiles, kl + kh, tile, tile), BF16),
+        vm((row_tiles, tile, width), F32), vm((nodes, width), BF16), vm((slots, nodes), BF16),
+        vm((n, share, width), BF16), vm((n, share, width), BF16), vm((row_tiles, tile, width), BF16),
+        vm((n * share // tile, tile, width), BF16), vm((slots, width), F32),
+        vm((nrep, ndom, 4 * width // ndom, own_cols), BF16),
+        vm((nrep, ndom, own_cols // ndom, span), BF16),
+        vm((1, 1, wide), F32), vm((n, 1, wide), F32),
+    ]
+    scratch += dma_sems(3, 1) + dma_sems(1, 1) + dma_sems(row_tiles, 2) + dma_sems(5, 1) + dma_sems(n, 4)
+    weight_sems = dma_sems(nrep, 2) + pairs(chips, nrep, 4)
+    scratch += weight_sems + weight_sems
+    scratch += [
         vm((slots, 4 * width), BF16), vm((4 * width, slots), BF16), vm((slots, hidden_units), F32),
         vm((slots, hidden_units), F32), vm((slots, own_cols), BF16), vm((hidden_units, span), F32),
         vm((4 * width, own_cols), F32), vm((1, 1, wide), F32), vm((n, 1, wide), F32),
@@ -588,20 +649,23 @@
     ]
     moment_sems = dma_sems(chips, 2) + dma_sems(peers, 4) + dma_sems(chips, 2)
     scratch += moment_sems + moment_sems + dma_sems(n, 2) + dma_sems(nrep, 2)
-    scratch += [pltpu.SemaphoreType.DMA((nrep, chips))] * 2 + dma_sems(nrep, 2)
+    scratch += pairs(nrep, chips, 2) + dma_sems(nrep, 2)
     scratch += dma_sems(1, 2) + dma_sems(chips, 2) + dma_sems(nrep, 2) + dma_sems(ndom, 2)
     vmem = pl.BlockSpec(memory_space=pltpu.VMEM)
-    first, second, turned = pl.pallas_call(
-        functools.partial(mlp_kernel, chunk, ndom, nrep, cores, classes),
-        out_shape=(sds((own_rows, own_cols), F32), sds((hidden_units // nrep, classes), F32),
-                   sds((1, wide), F32)),
-        in_specs=[vmem] * 7,
-        out_specs=(vmem, vmem, vmem),
+    smem = pl.BlockSpec(memory_space=pltpu.SMEM)
+    where = pl.BlockSpec(memory_space=pl.ANY)
+    next_hop, first, second, loss = pl.pallas_call(
+        functools.partial(step_kernel, chunk, ndom, nrep, cores, classes, kl, kh),
+        out_shape=(sds((nodes, width), BF16), sds((own_rows, own_cols), F32),
+                   sds((hidden_units // nrep, classes), F32), sds((1, n), F32)),
+        in_specs=[smem, smem, vmem, vmem] + [where] * 9,
+        out_specs=(vmem, vmem, vmem, vmem),
         scratch_shapes=scratch,
         compiler_params=pltpu.CompilerParams(collective_id=2, has_side_effects=True, vmem_limit_bytes=BIG),
-        name="mlp",
-    )(x3, tags, next_hop, w1, w2, counts, own_counts)
-    loss = turned[:, :n]
+        name="step",
+    )(local_cols, halo_cols, w_first, w_second, hop_feats, adj_local, adj_halo,
+      hop_feats.reshape(3, row_tiles, tile, width), boundary_rows,
+      train_ids, shuffle, labels[None], labelled[None])
     return (next_hop, loss, first, second)
 
 

time: 131 us -> 111 us (0.85)
  Pallas kernels: 111 us -> 101 us
  starting transfers between devices: 7.11 us -> 0 us
  local copies, waits for them, and re-layouts: 11.5 us -> 9.25 us
    pallas_call x4 -> x1, Pallas kernels: 111 us -> 101 us  [shards(): pl.pallas_call(functools.partial(step_kernel, chunk, ndom, nrep, cores, c...]
    ppermute x4 -> x0, starting transfers between devices: 7.11 us -> none  [the longest x3 7.04 us: send_rep(): lax.ppermute(half, 'rep', [(s, (s + o) % nrep) for s in range(nrep)])]
    unnamed x11 -> x6, local copies, waits for them, and re-layouts: 5.48 us -> 9.25 us
    another operation x2 -> x0, local copies, waits for them, and re-layouts: 2.91 us -> none  [the longest x1 2.05 us: shards(): shuffle[0][:, None]]
    slice x2 -> x0, local copies, waits for them, and re-layouts: 1.88 us -> none  [the longest x1 1.06 us: shards(): both[:, :, :h1].transpose(1, 0, 2, 3).reshape(nrep, cores * h1, own_cols)]
  transfers between devices with their start and end apart: 4 -> 0, of which waited for: 0 -> 0; matrix products, arithmetic and copies ran while one was open for 3% -> 0% of each run, Pallas kernels for 31% -> 0%
where the time goes in v2:
time: 111 us
  Pallas kernels  101 us (91%)
  local copies, waits for them, and re-layouts  9.25 us (8%)
    pallas_call x1, Pallas kernels, shards(): pl.pallas_call(functools.partial(step_kernel, chunk, ndom, nrep, cores, c...  101 us
    unnamed x6, local copies, waits for them, and re-layouts  9.25 us

profile of v2, /device:TPU:0, one launch (start us, length us, event | category | flops | bytes accessed | tf_op | source)
XLA Modules:
  0.0 111.0 jit_solution(10255754314968967734)
XLA Ops:
  0.6 1.4 %copy.16.hcols = s32[16,4]{1,0:T(8,128)} copy(s32[16,4]{0,1:T(4,128)} %param.16) | data formatting | bytes 512 | tf_op args[4]
  2.0 1.6 %copy.17.w2in = bf16[256,172]{1,0:T(8,128)(2,1)} copy(bf16[256,172]{0,1:T(8,128)(2,1)} %param.23) | data formatting | bytes 176128 | tf_op args[11]
  3.6 101.1 %step.1 = (bf16[2048,128]{1,0:T(8,128)(2,1)}, f32[64,256]{1,0:T(8,128)}, f32[256,172]{1,0:T(8,128)}, f32[1,32]{1,0:T(1,128)}) custom-call(s32[16,12]{1,0:T(8,128)} %lcols.1, s32[16,4]{1,0:T(8,128)} %copy.16.hcols, bf16[512,256]{1,0:T(8,128)(2,1)} %w1in.1, bf16[256,172]{1,0:T(8,128)(2,1)} %copy.17.w2in, bf16[3,2048,128]{2,1,0:T(8,128)(2,1)} %feats.1, ...), custom_call_target="tpu_custom_call" | custom-call | tf_op jit(solution)/shard_map/step/pallas_call | solution.py:657
  104.7 1.7 %copy.18 = f32[256,172]{0,1:T(8,128)} copy(f32[256,172]{1,0:T(8,128)} %get-tuple-element.15) | data formatting | bytes 352256
  106.4 1.9 %copy.22 = bf16[2048,128]{1,0:T(8,128)(2,1)} copy(bf16[2048,128]{1,0:T(8,128)(2,1)} %get-tuple-element.20) | data formatting | bytes 1048576
  108.3 1.2 %copy.23 = f32[1,32]{1,0:T(1,128)} copy(f32[1,32]{1,0:T(1,128)} %get-tuple-element.21) | data formatting | bytes 256
  109.5 1.5 %copy.24 = f32[64,256]{1,0:T(8,128)} copy(f32[64,256]{1,0:T(8,128)} %get-tuple-element.22) | data formatting | bytes 131072

commit v3 on v2

--- a/solution.py
+++ b/solution.py
@@ -25,9 +25,8 @@
 def step_kernel(chunk, ndom, nrep, cores, classes, kl, kh,
                lcols, hcols, w1in, w2in, feats, adj_l, adj_h, tiles, bound, ids, shuf, labels, labelled,
                next_out, first_out, second_out, loss_out,
-               ints, cols, order, whole, adjv, hacc, nh, pick, sent, halo, own_t, halo_t, tag, w1all, w2all, crow, cbuf,
-               f_s, t_s, a_s, b_s, i_s, c_s, c_r, p_s, p_r, uz_s, uz_r, up_s, up_r, uc_s, uc_r,
-               vz_s, vz_r, vp_s, vp_r, vc_s, vc_r,
+               ints, cols, order, whole, adjv, hacc, nh, pick, sent, halo, own_t, halo_t, tag, w1all, w2all, w2t, crow, cbuf,
+               f_s, t_s, a_s, b_s, i_s, c_s, c_r, p_s, p_r, u_s, v_s,
                xs, xt, zs, gs, dzs, g2acc, acc, lrow, lbuf,
                fsrc, fin, fpart, fall, fgath, bsrc, bin_, bpart, ball, bgath,
                gsrc, gin, gsum, gnear, gfar, gkeep, gfarin,
@@ -84,11 +83,16 @@
     def feat_copy(k):
         return pltpu.make_async_copy(feats.at[k], whole.at[:, k * fw:(k + 1) * fw], f_s.at[k])
 
-    def near_copy(i):
-        return pltpu.make_async_copy(adj_l.at[i], adjv.at[i, 0:kl], a_s.at[i])
-
-    def far_copy(i):
-        return pltpu.make_async_copy(adj_h.at[i], adjv.at[i, kl:kl + kh], b_s.at[i])
+    bands = a_s.shape[0]
+    deep = row_tiles // bands
+
+    def near_copy(j):
+        at = pl.ds(j * deep, deep)
+        return pltpu.make_async_copy(adj_l.at[at], adjv.at[at, 0:kl], a_s.at[j])
+
+    def far_copy(j):
+        at = pl.ds(j * deep, deep)
+        return pltpu.make_async_copy(adj_h.at[at], adjv.at[at, kl:kl + kh], b_s.at[j])
 
     given = (shuf, ids, labels, labelled, bound)
     int_copies = [pltpu.make_async_copy(ref, ints.at[m:m + 1, 0:ref.shape[1]], i_s.at[m])
@@ -100,13 +104,13 @@
     feat_copy(2).start()
     feat_copy(0).start()
     feat_copy(1).start()
-    each(row_tiles, lambda i: near_copy(i).start())
-    each(row_tiles, lambda i: far_copy(i).start())
+    each(bands, lambda j: near_copy(j).start())
+    each(bands, lambda j: far_copy(j).start())
 
     w1all[rep] = w1in[...].reshape(w1all.shape[1:])
-    w2pad = jnp.concatenate(
-        [w2in[...], jnp.zeros((w2in.shape[0], w2all.shape[3] - classes), BF16)], axis=1)
-    w2all[rep] = w2pad.reshape(w2all.shape[1:])
+    w2t[...] = jnp.zeros_like(w2t)
+    w2t[0:classes, :] = w2in[...].astype(F32)
+    w2all[rep] = w2t[...].T.astype(BF16).reshape(w2all.shape[1:])
     for copy in int_copies:
         copy.wait()
 
@@ -134,50 +138,6 @@
         rows = jnp.dot(spot, last, preferred_element_type=F32)
         count = LANES // share
         sent[m * count:(m + 1) * count] = rows.reshape(count, share, fw).astype(BF16)
-    pl.semaphore_wait(barrier, n - 1)
-
-    def send_halo(o):
-        peer = lax.rem(me + o, n)
-        return to(sent.at[peer], halo.at[me], p_s.at[o], p_r.at[o], peer // nrep, lax.rem(peer, nrep))
-
-    def spread_weights(buf, zsem, zrec, psem, prec, csem, crec):
-        def along(o):
-            return to(buf.at[rep, dom], buf.at[rep, dom], zsem.at[o], zrec.at[o], dom, lax.rem(rep + o, nrep))
-
-        def across(p, o):
-            at = lax.rem(rep + o, nrep)
-            return to(buf.at[at, dom], buf.at[at, dom], psem.at[p, o], prec.at[p, o],
-                      plane(p) * cores + core, rep)
-
-        def swap(p, o):
-            at = lax.rem(rep + o, nrep)
-            src = buf.at[at, lax.rem(chip - p + chips, chips) * cores + core]
-            return to(src, src, csem.at[p, o], crec.at[p, o], chip * cores + other, rep)
-
-        def each_pair(first, fn):
-            each(chips, lambda p: each(nrep, lambda o: fn(p, o), 1), first)
-
-        def stage(s):
-            if s == 0:
-                each(nrep, lambda o: along(o).start(), 1)
-            elif s == 1:
-                each(nrep, lambda o: along(o).wait(), 1)
-                each_pair(1, lambda p, o: across(p, o).start())
-                each(nrep, lambda o: swap(0, o).start(), 1)
-            elif s == 2:
-                each_pair(1, lambda p, o: across(p, o).wait())
-                each_pair(1, lambda p, o: swap(p, o).start())
-            else:
-                each_pair(0, lambda p, o: swap(p, o).wait())
-        return stage
-
-    w1_stage = spread_weights(w1all, uz_s, uz_r, up_s, up_r, uc_s, uc_r)
-    w2_stage = spread_weights(w2all, vz_s, vz_r, vp_s, vp_r, vc_s, vc_r)
-    each(n, lambda o: send_halo(o).start(), 1)
-    w1_stage(0)
-    w2_stage(0)
-    halo[me] = sent[me]
-
     lane = lax.broadcasted_iota(jnp.int32, (LANES, LANES), 1).astype(F32)
     table = cols[:, 2 * per_slot:4 * per_slot].astype(BF16)
     pair = lax.broadcasted_iota(jnp.int32, (LANES, 2 * per_slot), 1).astype(F32)
@@ -202,13 +162,70 @@
         at = rows_of(i)
         spot = one_hot(order[at, 0:1].astype(jnp.int32), nodes)
         pick[at, :] = spot
-        rows = jnp.dot(spot, whole[...], preferred_element_type=F32)
+        rows = jnp.dot(pick[at, :], whole[...], preferred_element_type=F32)
         xs[at, 0:3 * fw] = rows[:, 0:3 * fw].astype(BF16)
         tags = rows[:, 3 * fw:4 * fw]
         tag[at, :] = tags
         return own + jnp.sum(jnp.where(batch_rows(i), tags[:, 1:2], 0.0), axis=0, keepdims=True)
 
-    own_counts = lax.fori_loop(0, steps, gather_rows, jnp.zeros((1, crow.shape[2]), F32))
+    early = 2
+    own_counts = lax.fori_loop(0, early, gather_rows, jnp.zeros((1, crow.shape[2]), F32))
+    pl.semaphore_wait(barrier, n - 1)
+
+    def send_halo(o):
+        peer = lax.rem(me + o, n)
+        return to(sent.at[peer], halo.at[me], p_s.at[0], p_r.at[0], peer // nrep, lax.rem(peer, nrep))
+
+    def settle_all(src, dst, ssem, rsem):
+        to(src.at[pl.ds(0, n - 1)], dst.at[pl.ds(0, n - 1)], ssem.at[0], rsem.at[0],
+           chip * cores + other, rep).wait()
+
+    def spread_weights(buf, sems):
+        zsem, zrec, psem, prec, csem, crec = [sems.at[k] for k in range(6)]
+
+        def along(o):
+            return to(buf.at[rep, dom], buf.at[rep, dom], zsem, zrec, dom, lax.rem(rep + o, nrep))
+
+        def across(p, o):
+            at = lax.rem(rep + o, nrep)
+            return to(buf.at[at, dom], buf.at[at, dom], psem, prec, plane(p) * cores + core, rep)
+
+        def swap(p, o):
+            at = lax.rem(rep + o, nrep)
+            src = buf.at[at, lax.rem(chip - p + chips, chips) * cores + core]
+            return to(src, src, csem, crec, chip * cores + other, rep)
+
+        def each_pair(first, fn):
+            each(chips, lambda p: each(nrep, lambda o: fn(p, o), 1), first)
+
+        def settle(count, ssem, rsem):
+            if count <= ndom:
+                ref = buf.at[0, pl.ds(0, count)]
+            else:
+                ref = buf.at[pl.ds(0, nrep - 1), pl.ds(0, count // (nrep - 1))]
+            to(ref, ref, ssem, rsem, chip * cores + other, rep).wait()
+
+        def stage(s):
+            if s == 0:
+                each(nrep, lambda o: along(o).start(), 1)
+            elif s == 1:
+                settle(nrep - 1, zsem, zrec)
+                each_pair(1, lambda p, o: across(p, o).start())
+            elif s == 2:
+                settle((nrep - 1) * (chips - 1), psem, prec)
+                each_pair(0, lambda p, o: swap(p, o).start())
+            else:
+                settle((nrep - 1) * chips, csem, crec)
+        return stage
+
+    w1_stage = spread_weights(w1all, u_s)
+    w2_stage = spread_weights(w2all, v_s)
+    each(n, lambda o: send_halo(o).start(), 1)
+    w1_stage(0)
+    w2_stage(0)
+    halo[me] = sent[me]
+
+    own_counts = lax.fori_loop(early, steps, gather_rows, own_counts)
     w1_stage(1)
     w2_stage(1)
     crow[0] = own_counts
@@ -216,25 +233,29 @@
 
     def send_count(o):
         peer = lax.rem(me + o, n)
-        return to(crow.at[0], cbuf.at[me], c_s.at[o], c_r.at[o], peer // nrep, lax.rem(peer, nrep))
+        return to(crow.at[0], cbuf.at[me], c_s.at[0], c_r.at[0], peer // nrep, lax.rem(peer, nrep))
 
     each(n, lambda o: send_count(o).start(), 1)
 
     def hop_near(i):
-        near_copy(i).wait()
         left = jnp.concatenate([adjv[i, k] for k in range(kl)], axis=1)
         right = jnp.concatenate([own_t[lcols[i, k]] for k in range(kl)], axis=0)
         hacc[i] = jnp.dot(left, right, preferred_element_type=F32)
 
-    each(row_tiles, hop_near)
-    each(n, lambda o: send_halo(o).wait(), 1)
+    def near_band(j):
+        near_copy(j).wait()
+        each((j + 1) * deep, hop_near, j * deep)
+
+    each(bands, near_band)
+    settle_all(sent, halo, p_s, p_r)
     halo_t[...] = halo[...].reshape(halo_t.shape)
 
+    each(bands, lambda j: far_copy(j).wait())
+
     def hop_far(i):
-        far_copy(i).wait()
         left = jnp.concatenate([adjv[i, kl + k] for k in range(kh)], axis=1)
         right = jnp.concatenate(
-            [halo_t[hcols[i, k]] for k in range(kh)], axis=0)
+            [halo_t[hcols[k, i]] for k in range(kh)], axis=0)
         total = (hacc[i] + jnp.dot(left, right, preferred_element_type=F32)).astype(BF16)
         nh[pl.ds(pl.multiple_of(i * tile, tile), tile), :] = total
         next_out[pl.ds(pl.multiple_of(i * tile, tile), tile), :] = total
@@ -271,15 +292,15 @@
 
     def chip_sum(src, got, part, xs_, xr, combine):
         def swap(a):
-            return to(src.at[group_of(a, other)], got.at[a], xs_.at[a], xr.at[a],
-                      chip * cores + other, rep)
+            return to(src.at[group_of(a, other)], got.at[a], xs_.at[0], xr.at[0], chip * cores + other, rep)
 
         def start():
             each(chips, lambda a: swap(a).start())
 
         def finish():
+            to(part, got, xs_.at[0], xr.at[0], chip * cores + other, rep).wait()
+
             def one(a):
-                swap(a).wait()
                 part[a] = combine(src[group_of(a, core)], got[a])
             each(chips, one)
         return start, finish
@@ -290,38 +311,43 @@
     def scatter(part, arrived, as_, ar):
         def copy(o):
             a, r = walk(o)
-            return to(part.at[a, r], arrived.at[o], as_.at[o], ar.at[o], a * cores + core, r)
+            return to(part.at[a, r], arrived.at[o], as_.at[0], ar.at[0], a * cores + core, r)
 
         def start():
             each(peers, lambda o: copy(o).start(), 1)
             arrived[0] = part[chip, rep]
 
         def finish():
-            each(peers, lambda o: copy(o).wait(), 1)
+            span = arrived.at[pl.ds(0, peers - 1)]
+            to(span, span, as_.at[0], ar.at[0], chip * cores + other, rep).wait()
         return start, finish
 
     def gather(gath, gs_, gr, ws, wr):
         def copy(o):
             a, r = walk(o)
-            return to(gath.at[me], gath.at[me], gs_.at[o], gr.at[o], a * cores + core, r)
+            return to(gath.at[me], gath.at[me], gs_.at[0], gr.at[o // nrep], a * cores + core, r)
 
         def forward(da):
             at = group_of(lax.rem(chip + chips - da, chips), core)
-            return to(gath.at[at], gath.at[at], ws.at[da], wr.at[da], chip * cores + other, rep)
+            return to(gath.at[at], gath.at[at], ws.at[0], wr.at[0], chip * cores + other, rep)
+
+        def settle(count, ssem, rsem):
+            span = gath.at[pl.ds(0, count)]
+            return to(span, span, ssem, rsem, chip * cores + other, rep)
 
         def start():
             each(peers, lambda o: copy(o).start(), 1)
 
         def finish():
-            each(nrep, lambda o: copy(o).wait_recv(), 1)
+            settle(nrep - 1, gs_.at[0], gr.at[0]).wait_recv()
             forward(0).start()
 
             def chip_in(da):
-                each((da + 1) * nrep, lambda o: copy(o).wait_recv(), da * nrep)
+                settle(nrep, gs_.at[0], gr.at[da]).wait_recv()
                 forward(da).start()
             each(chips, chip_in, 1)
-            each(chips, lambda da: forward(da).wait())
-            each(peers, lambda o: copy(o).wait_send(), 1)
+            settle(peers, ws.at[0], wr.at[0]).wait()
+            settle(peers - 1, gs_.at[0], gr.at[0]).wait_send()
         return start, finish
 
     def both_moments(a, b):
@@ -346,10 +372,9 @@
     fgath[me] = jnp.concatenate([mu, lax.rsqrt(m2 * (1.0 / (n * chunk)) + 1e-05)], axis=0)
     start, finish = gather(fgath, fg_s, fg_r, fw_s, fw_r)
     start()
-    g2acc[...] = jnp.zeros_like(g2acc)
     loss_row = jnp.zeros((1, lrow.shape[2]), F32)
     w2_stage(3)
-    each(n, lambda o: send_count(o).wait(), 1)
+    settle_all(cbuf, cbuf, c_s, c_r)
     counts = jnp.maximum(jnp.sum(cbuf[...], axis=0), 1.0)
     finish()
 
@@ -364,8 +389,8 @@
         rstd = jnp.concatenate([st[:, half + j:half + j + 1] for j in range(half)], axis=2)
         normed = ((z3 - mean) * rstd).reshape(block, hidden_units)
         zs[at, :] = normed
-        hidden = jnp.maximum(normed, 0.0).astype(BF16)
-        logits = jnp.dot(hidden, second, preferred_element_type=F32)
+        pick[at, 0:hidden_units] = jnp.maximum(normed, 0.0).astype(BF16)
+        logits = jnp.dot(pick[at, 0:hidden_units], second, preferred_element_type=F32)
         lane = lax.broadcasted_iota(jnp.int32, logits.shape, 1)
         logits = jnp.where(lane < classes, logits, -1e30)
         row_max = jnp.max(logits, axis=1, keepdims=True)
@@ -378,15 +403,19 @@
         mine = batch_rows(i)
         count = jnp.sum(jnp.where(mine, counts, 0.0), axis=1, keepdims=True)
         dlogits = ((expos / totals - onehot) * (mark / count)).astype(BF16)
-        g2acc[...] += lax.dot_general(hidden, dlogits, (((0,), (0,)), ((), ())), preferred_element_type=F32)
-        masked = jnp.where(normed > 0, by_lanes(dlogits, second), 0.0)
-        gs[at, :] = masked
-        sums = jnp.sum(masked.reshape(groups, chunk, hidden_units), axis=1, keepdims=True)
-        projs = jnp.sum((masked * normed).reshape(groups, chunk, hidden_units), axis=1, keepdims=True)
-        for j in range(half):
-            cut = slice(j * 128, (j + 1) * 128)
-            bsrc[here, j:j + 1] = sums[:, :, cut]
-            bsrc[here, half + j:half + j + 1] = projs[:, :, cut]
+        pick[at, hidden_units:hidden_units + dlogits.shape[1]] = dlogits
+        for r in range(nrep):
+            span = slice(r * width, (r + 1) * width)
+            seen = zs[at, span]
+            back = by_lanes(dlogits, second[span])
+            masked = jnp.where(seen > 0, back, 0.0)
+            gs[at, span] = masked
+            sums = jnp.sum(masked.reshape(groups, chunk, width), axis=1, keepdims=True)
+            projs = jnp.sum((masked * seen).reshape(groups, chunk, width), axis=1, keepdims=True)
+            for j in range(per):
+                cut = slice(j * 128, (j + 1) * 128)
+                bsrc[here, r * per + j:r * per + j + 1] = sums[:, :, cut]
+                bsrc[here, half + r * per + j:half + r * per + j + 1] = projs[:, :, cut]
         return loss_row + jnp.sum(jnp.where(mine, mark * cross, 0.0), axis=0, keepdims=True)
 
     loss_row = lax.fori_loop(0, steps, head, loss_row)
@@ -398,27 +427,16 @@
 
     def send_loss(o):
         peer = lax.rem(me + o, n)
-        return to(lrow.at[0], lbuf.at[me], l_s.at[o], l_r.at[o], peer // nrep, lax.rem(peer, nrep))
+        return to(lrow.at[0], lbuf.at[me], l_s.at[0], l_r.at[0], peer // nrep, lax.rem(peer, nrep))
 
     part = hsrc.shape[3]
     for r in range(nrep):
+        g2acc[r * width:(r + 1) * width, :] = lax.dot_general(
+            pick[:, r * width:(r + 1) * width], pick[:, hidden_units:hidden_units + g2acc.shape[1]],
+            (((0,), (0,)), ((), ())), preferred_element_type=F32)
         for d in range(ndom):
             first_row = (r * ndom + d) * part
             hsrc[d % cores, d // cores, r] = g2acc[first_row:first_row + part, :].astype(BF16)
-    h_swap = to(hsrc.at[other], hin, hx_s.at[0], hx_r.at[0], chip * cores + other, rep)
-    h_swap.start()
-    finish()
-    start, finish = scatter(bpart, ball, ba_s, ba_r)
-    start()
-    h_swap.wait()
-    hsum[...] = (hsrc[core].astype(F32) + hin[...].astype(F32)).astype(BF16)
-    finish()
-    bgath[me] = jnp.sum(ball[...], axis=0) * (1.0 / (n * chunk))
-    start, finish = gather(bgath, bg_s, bg_r, bw_s, bw_r)
-    start()
-    each(n, lambda o: send_loss(o).start(), 1)
-    finish()
-
     def h_near(o):
         return to(hsum.at[plane(o)], hnear.at[o - 1], hn_s.at[o], hn_r.at[o], plane(o) * cores + core, rep)
 
@@ -449,8 +467,24 @@
             each(ndom, lambda o: h_round(o).start(), 1)
         else:
             each(ndom, lambda o: h_round(o).wait(), 1)
-            for d in range(ndom):
-                second_out[d * part:(d + 1) * part, :] = hgath[d][:, :classes]
+            both = hgath[...].reshape(ndom * part, hgath.shape[2]).T
+            second_out[...] = both[:classes]
+
+    h_swap = to(hsrc.at[other], hin, hx_s.at[0], hx_r.at[0], chip * cores + other, rep)
+    h_swap.start()
+    finish()
+    start, finish = scatter(bpart, ball, ba_s, ba_r)
+    start()
+    h_swap.wait()
+    hsum[...] = (hsrc[core].astype(F32) + hin[...].astype(F32)).astype(BF16)
+    h_stage(0)
+    finish()
+    bgath[me] = jnp.sum(ball[...], axis=0) * (1.0 / (n * chunk))
+    start, finish = gather(bgath, bg_s, bg_r, bw_s, bw_r)
+    start()
+    each(n, lambda o: send_loss(o).start(), 1)
+    h_stage(1)
+    finish()
 
     high = acc.shape[0] // ndom
 
@@ -507,19 +541,21 @@
             gsrc[r, d % cores, d // cores] = acc[d * high:(d + 1) * high, :].astype(BF16)
 
     for r in range(nrep):
-        h_stage(r) if r < 4 else None
         tail(r)
+        if r == 1:
+            h_stage(2)
         g_stage(r, 0)
         if r >= 1:
             g_stage(r - 1, 1)
         if r >= 2:
             g_stage(r - 2, 2)
-    for s in range(nrep, 4):
-        h_stage(s)
+    if nrep < 2:
+        h_stage(2)
     g_stage(nrep - 1, 1)
     if nrep >= 2:
         g_stage(nrep - 2, 2)
-    each(n, lambda o: send_loss(o).wait(), 1)
+    h_stage(3)
+    settle_all(lbuf, lbuf, l_s, l_r)
     losses = lbuf[...]
     source = lax.broadcasted_iota(jnp.int32, losses.shape, 0)
     lane = lax.broadcasted_iota(jnp.int32, losses.shape, 2)
@@ -584,6 +620,12 @@
 
     here = batch_lanes(rows, cnt_out.shape[1], chunk)
     cnt_out[...] += jnp.sum(jnp.where(here, tags[:, 1:2], 0.0), axis=0, keepdims=True)
+
+
+def emit_kernel(*refs):
+    count = len(refs) // 2
+    for source, target in zip(refs[:count], refs[count:]):
+        target[...] = source[...]
 
 
 def dma_sems(n, count):
@@ -629,11 +671,11 @@
         vm((n * share // tile, tile, width), BF16), vm((slots, width), F32),
         vm((nrep, ndom, 4 * width // ndom, own_cols), BF16),
         vm((nrep, ndom, own_cols // ndom, span), BF16),
-        vm((1, 1, wide), F32), vm((n, 1, wide), F32),
+        vm((span, own_cols), F32), vm((1, 1, wide), F32), vm((n, 1, wide), F32),
     ]
-    scratch += dma_sems(3, 1) + dma_sems(1, 1) + dma_sems(row_tiles, 2) + dma_sems(5, 1) + dma_sems(n, 4)
-    weight_sems = dma_sems(nrep, 2) + pairs(chips, nrep, 4)
-    scratch += weight_sems + weight_sems
+    bands = 4 if row_tiles % 4 == 0 else row_tiles
+    scratch += dma_sems(3, 1) + dma_sems(1, 1) + dma_sems(bands, 2) + dma_sems(5, 1) + dma_sems(1, 4)
+    scratch += dma_sems(6, 2)
     scratch += [
         vm((slots, 4 * width), BF16), vm((4 * width, slots), BF16), vm((slots, hidden_units), F32),
         vm((slots, hidden_units), F32), vm((slots, own_cols), BF16), vm((hidden_units, span), F32),
@@ -647,8 +689,8 @@
         vm((nrep,) + half_block, F32), vm((nrep,) + half_block, BF16), vm((nrep - 1,) + half_block, BF16),
         vm((ndom,) + half_block, F32),
     ]
-    moment_sems = dma_sems(chips, 2) + dma_sems(peers, 4) + dma_sems(chips, 2)
-    scratch += moment_sems + moment_sems + dma_sems(n, 2) + dma_sems(nrep, 2)
+    moment_sems = dma_sems(1, 5) + dma_sems(chips, 1) + dma_sems(1, 2)
+    scratch += moment_sems + moment_sems + dma_sems(1, 2) + dma_sems(nrep, 2)
     scratch += pairs(nrep, chips, 2) + dma_sems(nrep, 2)
     scratch += dma_sems(1, 2) + dma_sems(chips, 2) + dma_sems(nrep, 2) + dma_sems(ndom, 2)
     vmem = pl.BlockSpec(memory_space=pltpu.VMEM)
@@ -657,16 +699,26 @@
     next_hop, first, second, loss = pl.pallas_call(
         functools.partial(step_kernel, chunk, ndom, nrep, cores, classes, kl, kh),
         out_shape=(sds((nodes, width), BF16), sds((own_rows, own_cols), F32),
-                   sds((hidden_units // nrep, classes), F32), sds((1, n), F32)),
+                   sds((classes, own_cols), F32), sds((1, n), F32)),
         in_specs=[smem, smem, vmem, vmem] + [where] * 9,
         out_specs=(vmem, vmem, vmem, vmem),
         scratch_shapes=scratch,
         compiler_params=pltpu.CompilerParams(collective_id=2, has_side_effects=True, vmem_limit_bytes=BIG),
         name="step",
-    )(local_cols, halo_cols, w_first, w_second, hop_feats, adj_local, adj_halo,
+    )(local_cols, halo_cols.T, w_first, w_second.T, hop_feats, adj_local, adj_halo,
       hop_feats.reshape(3, row_tiles, tile, width), boundary_rows,
       train_ids, shuffle, labels[None], labelled[None])
-    return (next_hop, loss, first, second)
+    done = (next_hop, loss, first, second)
+    specs = [pl.BlockSpec(v.shape, lambda i: (0, 0)) for v in done]
+    next_hop, loss, first, second = pl.pallas_call(
+        emit_kernel,
+        out_shape=tuple(sds(v.shape, v.dtype) for v in done),
+        grid=(1,),
+        in_specs=specs,
+        out_specs=tuple(specs),
+        name="emit",
+    )(*done)
+    return (next_hop, loss, first, second.T)
 
 
 def solution(mesh):

time: 111 us -> 95.5 us (0.86)
  local copies, waits for them, and re-layouts: 9.25 us -> 0 us
  Pallas kernels: 101 us -> 94.7 us
    unnamed x6 -> x0, local copies, waits for them, and re-layouts: 9.25 us -> none
    pallas_call x1, Pallas kernels: 101 us -> 92.7 us  [shards(): pl.pallas_call(functools.partial(step_kernel, chunk, ndom, nrep, cores, c...]
    pallas_call x0 -> x1, Pallas kernels: none -> 2.01 us  [shards(): pl.pallas_call(emit_kernel, out_shape=tuple((sds(v.shape, v.dtype) for v...]
where the time goes in v3:
time: 95.5 us; the launch traced here: 95.3 us
  Pallas kernels  94.7 us (99%)
    pallas_call x1, Pallas kernels, shards(): pl.pallas_call(functools.partial(step_kernel, chunk, ndom, nrep, cores, c...  92.7 us
    pallas_call x1, Pallas kernels, shards(): pl.pallas_call(emit_kernel, out_shape=tuple((sds(v.shape, v.dtype) for v...  2.01 us

profile of v3, /device:TPU:0, one launch (start us, length us, event | category | flops | bytes accessed | tf_op | source)
XLA Modules:
  0.0 95.3 jit_solution(13633845539044913388)
XLA Ops:
  0.6 92.7 %step.1 = (bf16[2048,128]{1,0:T(8,128)(2,1)}, f32[64,256]{1,0:T(8,128)}, f32[172,256]{1,0:T(8,128)}, f32[1,32]{1,0:T(1,128)}) custom-call(s32[16,12]{1,0:T(8,128)} %lcols.1, s32[4,16]{1,0:T(4,128)} %bitcast.10, bf16[512,256]{1,0:T(8,128)(2,1)} %w1in.1, bf16[172,256]{1,0:T(8,128)(2,1)} %bitcast.7, bf16[3,2048,128]{2,1,0:T(8,128)(2,1)} %feats.1, ...), custom_call_target="tpu_custom_call" | custom-call | tf_op jit(solution)/shard_map/step/pallas_call | solution.py:699
  93.3 2.0 %emit.1 = (bf16[2048,128]{1,0:T(8,128)(2,1)}, f32[1,32]{1,0:T(1,128)}, f32[64,256]{1,0:T(8,128)}, f32[172,256]{1,0:T(8,128)}) custom-call(bf16[2048,128]{1,0:T(8,128)(2,1)} %get-tuple-element.12.refs_0_, f32[1,32]{1,0:T(1,128)} %get-tuple-element.13.refs_1_, f32[64,256]{1,0:T(8,128)} %get-tuple-element.14.refs_2_, f32[172,256]{1,0:T(8,128)} %get-tuple-element.15.refs_3_), custom_call_target="tpu_custom_call" | custom-call | tf_op jit(solution)/shard_map/emit/pallas_call | solution.py:713

commit v4 on v3

--- a/solution.py
+++ b/solution.py
@@ -154,19 +154,21 @@
     for k in range(3):
         feat_copy(k).wait()
 
-    def batch_rows(i):
-        rows_at = i * block + lax.broadcasted_iota(jnp.int32, (block, crow.shape[2]), 0)
-        return rows_at // chunk == lax.broadcasted_iota(jnp.int32, (block, crow.shape[2]), 1)
+    def batch_rows(i, count):
+        rows_at = i * count + lax.broadcasted_iota(jnp.int32, (count, crow.shape[2]), 0)
+        return rows_at // chunk == lax.broadcasted_iota(jnp.int32, (count, crow.shape[2]), 1)
 
     def gather_rows(i, own):
         at = rows_of(i)
-        spot = one_hot(order[at, 0:1].astype(jnp.int32), nodes)
-        pick[at, :] = spot
+        spot = order[at, 0:1].astype(jnp.int32)
+        strip = 2 * LANES
+        for j in range(nodes // strip):
+            pick[at, j * strip:(j + 1) * strip] = one_hot(spot - j * strip, strip)
         rows = jnp.dot(pick[at, :], whole[...], preferred_element_type=F32)
         xs[at, 0:3 * fw] = rows[:, 0:3 * fw].astype(BF16)
         tags = rows[:, 3 * fw:4 * fw]
         tag[at, :] = tags
-        return own + jnp.sum(jnp.where(batch_rows(i), tags[:, 1:2], 0.0), axis=0, keepdims=True)
+        return own + jnp.sum(jnp.where(batch_rows(i, block), tags[:, 1:2], 0.0), axis=0, keepdims=True)
 
     early = 2
     own_counts = lax.fori_loop(0, early, gather_rows, jnp.zeros((1, crow.shape[2]), F32))
@@ -227,7 +229,6 @@
 
     own_counts = lax.fori_loop(early, steps, gather_rows, own_counts)
     w1_stage(1)
-    w2_stage(1)
     crow[0] = own_counts
     cbuf[me] = own_counts
 
@@ -262,7 +263,7 @@
 
     each(row_tiles, hop_far)
     w1_stage(2)
-    w2_stage(2)
+    w2_stage(1)
 
     def gather_next(i):
         at = rows_of(i)
@@ -289,6 +290,7 @@
                 fsrc[here, half + r * per + j:half + r * per + j + 1] = spread2[:, :, cut]
 
     each(steps, pre)
+    w2_stage(2)
 
     def chip_sum(src, got, part, xs_, xr, combine):
         def swap(a):
@@ -378,18 +380,24 @@
     counts = jnp.maximum(jnp.sum(cbuf[...], axis=0), 1.0)
     finish()
 
-    second = w2all[...].reshape(hidden_units, w2all.shape[3])
-
-    def head(i, loss_row):
-        at = pl.ds(pl.multiple_of(i * block, block), block)
-        here = pl.ds(i * groups, groups)
-        z3 = zs[at, :].reshape(groups, chunk, hidden_units)
+
+    few = block
+    some = few // chunk
+
+    def head_rows(i):
+        at = pl.ds(pl.multiple_of(i * few, few), few)
+        here = pl.ds(i * some, some)
         st = fgath[here]
-        mean = jnp.concatenate([st[:, j:j + 1] for j in range(half)], axis=2)
-        rstd = jnp.concatenate([st[:, half + j:half + j + 1] for j in range(half)], axis=2)
-        normed = ((z3 - mean) * rstd).reshape(block, hidden_units)
-        zs[at, :] = normed
-        pick[at, 0:hidden_units] = jnp.maximum(normed, 0.0).astype(BF16)
+        for r in range(nrep):
+            span = slice(r * width, (r + 1) * width)
+            z3 = zs[at, span].reshape(some, chunk, width)
+            mean = jnp.concatenate([st[:, r * per + j:r * per + j + 1] for j in range(per)], axis=2)
+            rstd = jnp.concatenate(
+                [st[:, half + r * per + j:half + r * per + j + 1] for j in range(per)], axis=2)
+            normed = ((z3 - mean) * rstd).reshape(few, width)
+            zs[at, span] = normed
+            pick[at, span] = jnp.maximum(normed, 0.0).astype(BF16)
+        second = w2all[...].reshape(hidden_units, w2all.shape[3])
         logits = jnp.dot(pick[at, 0:hidden_units], second, preferred_element_type=F32)
         lane = lax.broadcasted_iota(jnp.int32, logits.shape, 1)
         logits = jnp.where(lane < classes, logits, -1e30)
@@ -400,23 +408,28 @@
         mark = tag[at, 1:2]
         onehot = (lane == target).astype(F32)
         cross = jnp.log(totals) + row_max - jnp.sum(onehot * logits, axis=1, keepdims=True)
-        mine = batch_rows(i)
+        mine = batch_rows(i, few)
         count = jnp.sum(jnp.where(mine, counts, 0.0), axis=1, keepdims=True)
         dlogits = ((expos / totals - onehot) * (mark / count)).astype(BF16)
         pick[at, hidden_units:hidden_units + dlogits.shape[1]] = dlogits
         for r in range(nrep):
             span = slice(r * width, (r + 1) * width)
             seen = zs[at, span]
-            back = by_lanes(dlogits, second[span])
+            back = by_lanes(dlogits, w2all[r].reshape(width, w2all.shape[3]))
             masked = jnp.where(seen > 0, back, 0.0)
             gs[at, span] = masked
-            sums = jnp.sum(masked.reshape(groups, chunk, width), axis=1, keepdims=True)
-            projs = jnp.sum((masked * seen).reshape(groups, chunk, width), axis=1, keepdims=True)
+            sums = jnp.sum(masked.reshape(some, chunk, width), axis=1, keepdims=True)
+            projs = jnp.sum((masked * seen).reshape(some, chunk, width), axis=1, keepdims=True)
             for j in range(per):
                 cut = slice(j * 128, (j + 1) * 128)
                 bsrc[here, r * per + j:r * per + j + 1] = sums[:, :, cut]
                 bsrc[here, half + r * per + j:half + r * per + j + 1] = projs[:, :, cut]
-        return loss_row + jnp.sum(jnp.where(mine, mark * cross, 0.0), axis=0, keepdims=True)
+        return jnp.sum(jnp.where(mine, mark * cross, 0.0), axis=0, keepdims=True)
+
+    def head(i, loss_row):
+        for k in range(block // few):
+            loss_row = loss_row + head_rows(i * (block // few) + k)
+        return loss_row
 
     loss_row = lax.fori_loop(0, steps, head, loss_row)
     start, finish = chip_sum(bsrc, bin_, bpart, bx_s, bx_r, lambda a, b: a + b)
@@ -541,16 +554,14 @@
             gsrc[r, d % cores, d // cores] = acc[d * high:(d + 1) * high, :].astype(BF16)
 
     for r in range(nrep):
+        if r == 0:
+            h_stage(2)
         tail(r)
-        if r == 1:
-            h_stage(2)
         g_stage(r, 0)
         if r >= 1:
             g_stage(r - 1, 1)
         if r >= 2:
             g_stage(r - 2, 2)
-    if nrep < 2:
-        h_stage(2)
     g_stage(nrep - 1, 1)
     if nrep >= 2:
         g_stage(nrep - 2, 2)

time: 95.5 us -> 92 us (0.963)
  Pallas kernels: 94.7 us -> 91.1 us
    pallas_call x1, Pallas kernels: 92.7 us -> 89.1 us  [shards(): pl.pallas_call(functools.partial(step_kernel, chunk, ndom, nrep, cores, c...]
where the time goes in v4:
time: 92 us; the launch traced here: 91.8 us
  Pallas kernels  91.1 us (99%)
    pallas_call x1, Pallas kernels, shards(): pl.pallas_call(functools.partial(step_kernel, chunk, ndom, nrep, cores, c...  89.1 us
    pallas_call x1, Pallas kernels, shards(): pl.pallas_call(emit_kernel, out_shape=tuple((sds(v.shape, v.dtype) for v...  2.01 us

profile of v4, /device:TPU:0, one launch (start us, length us, event | category | flops | bytes accessed | tf_op | source)
XLA Modules:
  0.0 91.8 jit_solution(4734636904698784493)
XLA Ops:
  0.6 89.1 %step.1 = (bf16[2048,128]{1,0:T(8,128)(2,1)}, f32[64,256]{1,0:T(8,128)}, f32[172,256]{1,0:T(8,128)}, f32[1,32]{1,0:T(1,128)}) custom-call(s32[16,12]{1,0:T(8,128)} %lcols.1, s32[4,16]{1,0:T(4,128)} %bitcast.10, bf16[512,256]{1,0:T(8,128)(2,1)} %w1in.1, bf16[172,256]{1,0:T(8,128)(2,1)} %bitcast.7, bf16[3,2048,128]{2,1,0:T(8,128)(2,1)} %feats.1, ...), custom_call_target="tpu_custom_call" | custom-call | tf_op jit(solution)/shard_map/step/pallas_call | solution.py:710
  89.8 2.0 %emit.1 = (bf16[2048,128]{1,0:T(8,128)(2,1)}, f32[1,32]{1,0:T(1,128)}, f32[64,256]{1,0:T(8,128)}, f32[172,256]{1,0:T(8,128)}) custom-call(bf16[2048,128]{1,0:T(8,128)(2,1)} %get-tuple-element.12.refs_0_, f32[1,32]{1,0:T(1,128)} %get-tuple-element.13.refs_1_, f32[64,256]{1,0:T(8,128)} %get-tuple-element.14.refs_2_, f32[172,256]{1,0:T(8,128)} %get-tuple-element.15.refs_3_), custom_call_target="tpu_custom_call" | custom-call | tf_op jit(solution)/shard_map/emit/pallas_call | solution.py:724

commit v5 on v4

--- a/solution.py
+++ b/solution.py
@@ -170,7 +170,7 @@
         tag[at, :] = tags
         return own + jnp.sum(jnp.where(batch_rows(i, block), tags[:, 1:2], 0.0), axis=0, keepdims=True)
 
-    early = 2
+    early = 0
     own_counts = lax.fori_loop(0, early, gather_rows, jnp.zeros((1, crow.shape[2]), F32))
     pl.semaphore_wait(barrier, n - 1)
 

time: 92 us -> 90.2 us (0.980)
  Pallas kernels: 91.1 us -> 89.3 us
    pallas_call x1, Pallas kernels: 89.1 us -> 87.3 us  [shards(): pl.pallas_call(functools.partial(step_kernel, chunk, ndom, nrep, cores, c...]
where the time goes in v5:
time: 90.2 us; the launch traced here: 90 us
  Pallas kernels  89.3 us (99%)
    pallas_call x1, Pallas kernels, shards(): pl.pallas_call(functools.partial(step_kernel, chunk, ndom, nrep, cores, c...  87.3 us
    pallas_call x1, Pallas kernels, shards(): pl.pallas_call(emit_kernel, out_shape=tuple((sds(v.shape, v.dtype) for v...  2.01 us

profile of v5, /device:TPU:0, one launch (start us, length us, event | category | flops | bytes accessed | tf_op | source)
XLA Modules:
  0.0 90.0 jit_solution(18423237176132711977)
XLA Ops:
  0.6 87.3 %step.1 = (bf16[2048,128]{1,0:T(8,128)(2,1)}, f32[64,256]{1,0:T(8,128)}, f32[172,256]{1,0:T(8,128)}, f32[1,32]{1,0:T(1,128)}) custom-call(s32[16,12]{1,0:T(8,128)} %lcols.1, s32[4,16]{1,0:T(4,128)} %bitcast.10, bf16[512,256]{1,0:T(8,128)(2,1)} %w1in.1, bf16[172,256]{1,0:T(8,128)(2,1)} %bitcast.7, bf16[3,2048,128]{2,1,0:T(8,128)(2,1)} %feats.1, ...), custom_call_target="tpu_custom_call" | custom-call | tf_op jit(solution)/shard_map/step/pallas_call | solution.py:710
  88.0 2.0 %emit.1 = (bf16[2048,128]{1,0:T(8,128)(2,1)}, f32[1,32]{1,0:T(1,128)}, f32[64,256]{1,0:T(8,128)}, f32[172,256]{1,0:T(8,128)}) custom-call(bf16[2048,128]{1,0:T(8,128)(2,1)} %get-tuple-element.12.refs_0_, f32[1,32]{1,0:T(1,128)} %get-tuple-element.13.refs_1_, f32[64,256]{1,0:T(8,128)} %get-tuple-element.14.refs_2_, f32[172,256]{1,0:T(8,128)} %get-tuple-element.15.refs_3_), custom_call_target="tpu_custom_call" | custom-call | tf_op jit(solution)/shard_map/emit/pallas_call | solution.py:724
